TPU v7x, 32 devices: a 4x2x2 block of a 4x4x8 slice. The times are simulated.
32 devices in a mesh: dp: 4 (over y, z), tp: 8 (over x, core).
Axes of the slice: x: 4, y: 2, z: 2, core: 2. Of those that a mesh axis runs over, the one named last changes fastest.
The devices are a block of a 4x4x8 slice.
Arguments:
- x_in: bfloat16 [4, 3072, 3840], P('dp', 'tp'), parts along dimension 0
- positions: int32 [4, 3072], P('dp', 'tp'), parts along dimension 0
- grad_out: bfloat16 [4, 3072, 3840], P('dp', 'tp'), parts along dimension 0
- w_query: bfloat16 [3840, 16, 256], P(None, 'tp')
- w_key: bfloat16 [3840, 8, 256], P(None, 'tp')
- w_value: bfloat16 [3840, 8, 256], P(None, 'tp')
- w_out: bfloat16 [16, 256, 3840], P('tp')
- gain_pre: float32 [3840], replicated
- gain_post: float32 [3840], replicated
Outputs:
- output 1: bfloat16 [4, 3072, 3840], P('dp', 'tp'), parts along dimension 0
- output 2: bfloat16 [4, 3072, 3840], P('dp', 'tp'), parts along dimension 0
- output 3: float32 [15360, 16, 256], P('dp', 'tp'), parts along dimension 0
- output 4: float32 [15360, 8, 256], P('dp', 'tp'), parts along dimension 0
- output 5: float32 [15360, 8, 256], P('dp', 'tp'), parts along dimension 0
- output 6: float32 [64, 256, 3840], P(('dp', 'tp')), parts along dimension 0
- output 7: float32 [15360], P('dp'), parts along dimension 0
- output 8: float32 [15360], P('dp'), parts along dimension 0
There are 4 independent parts. A program takes and returns all parts, laid end to end along the dimension named above; an argument that names none is the same for every part.
All inputs are finite; a program needn't handle non-finite values.
Results may differ from a plain program's by a relative error of at most 0.0190443.
Values are sent between devices in bfloat16 or wider.
A program may use at most 768 MiB of HBM per device.

v0:
```python
import jax
import jax.numpy as jnp
from jax import lax
from jax.sharding import PartitionSpec as P

WINDOW = 4096
SOFT_CAP = 50.0
NORM_EPS = 1e-6
ROPE_THETA = 10000.0


def rms_norm(hidden, scale_w):
    values = hidden.astype(jnp.float32)
    inv_rms = lax.rsqrt(jnp.mean(values * values, axis=-1, keepdims=True) + NORM_EPS)
    return (values * inv_rms * (1.0 + scale_w)).astype(jnp.bfloat16)


def rope_tables(positions, head_dim):
    half_dim = head_dim // 2
    inv_freq = ROPE_THETA ** (-2.0 * jnp.arange(half_dim, dtype=jnp.float32) / head_dim)
    angles = positions.astype(jnp.float32)[:, :, None] * inv_freq
    return jnp.cos(angles)[:, :, None, :], jnp.sin(angles)[:, :, None, :]


def apply_rope(values, cos_t, sin_t):
    half_dim = values.shape[-1] // 2
    lo_half = values[..., :half_dim]
    hi_half = values[..., half_dim:]
    return jnp.concatenate([lo_half * cos_t - hi_half * sin_t, hi_half * cos_t + lo_half * sin_t], axis=-1)


def rope_transpose(grad_in, cos_t, sin_t):
    half_dim = grad_in.shape[-1] // 2
    lo_half = grad_in[..., :half_dim]
    hi_half = grad_in[..., half_dim:]
    return jnp.concatenate([lo_half * cos_t + hi_half * sin_t, hi_half * cos_t - lo_half * sin_t], axis=-1)


def block_probs(q_blk, k_blk, pos_q, pos_k):
    scores = jnp.einsum('bqkgd,bskd->bkgqs', q_blk, k_blk, preferred_element_type=jnp.float32)
    capped = SOFT_CAP * jnp.tanh(scores / SOFT_CAP)
    pos_gap = pos_q[:, :, None] - pos_k[:, None, :]
    in_window = ((pos_gap >= 0) & (pos_gap < WINDOW))[:, None, None, :, :]
    return capped, jax.nn.softmax(jnp.where(in_window, capped, -1e30), axis=-1)


def attention_fwd(q_all, k_all, v_all, positions):
    seq_len = positions.shape[1]
    q_block = min(128, seq_len)
    slab_len = min(WINDOW + q_block, seq_len)

    def block_step(blk_idx, out_acc):
        q_start = blk_idx * q_block
        k_start = jnp.maximum(q_start + q_block - slab_len, 0)
        q_blk = lax.dynamic_slice_in_dim(q_all, q_start, q_block, axis=1)
        k_blk = lax.dynamic_slice_in_dim(k_all, k_start, slab_len, axis=1)
        v_blk = lax.dynamic_slice_in_dim(v_all, k_start, slab_len, axis=1)
        pos_q = lax.dynamic_slice_in_dim(positions, q_start, q_block, axis=1)
        pos_k = lax.dynamic_slice_in_dim(positions, k_start, slab_len, axis=1)
        prob_blk = block_probs(q_blk, k_blk, pos_q, pos_k)[1]
        out_blk = jnp.einsum('bkgqs,bskd->bqkgd', prob_blk.astype(jnp.bfloat16), v_blk, preferred_element_type=jnp.float32)
        return lax.dynamic_update_slice_in_dim(out_acc, out_blk.astype(jnp.bfloat16), q_start, axis=1)

    return lax.fori_loop(0, seq_len // q_block, block_step, jnp.zeros_like(q_all))


def attention_bwd(q_all, k_all, v_all, positions, d_out):
    seq_len = positions.shape[1]
    q_block = min(128, seq_len)
    slab_len = min(WINDOW + q_block, seq_len)

    def block_step(blk_idx, grad_acc):
        d_q, d_k, d_v = grad_acc
        q_start = blk_idx * q_block
        k_start = jnp.maximum(q_start + q_block - slab_len, 0)
        q_blk = lax.dynamic_slice_in_dim(q_all, q_start, q_block, axis=1)
        k_blk = lax.dynamic_slice_in_dim(k_all, k_start, slab_len, axis=1)
        v_blk = lax.dynamic_slice_in_dim(v_all, k_start, slab_len, axis=1)
        do_blk = lax.dynamic_slice_in_dim(d_out, q_start, q_block, axis=1)
        pos_q = lax.dynamic_slice_in_dim(positions, q_start, q_block, axis=1)
        pos_k = lax.dynamic_slice_in_dim(positions, k_start, slab_len, axis=1)
        capped, prob_blk = block_probs(q_blk, k_blk, pos_q, pos_k)
        d_prob = jnp.einsum('bqkgd,bskd->bkgqs', do_blk, v_blk, preferred_element_type=jnp.float32)
        dv_blk = jnp.einsum('bkgqs,bqkgd->bskd', prob_blk.astype(jnp.bfloat16), do_blk, preferred_element_type=jnp.float32)
        d_capped = prob_blk * (d_prob - jnp.sum(prob_blk * d_prob, axis=-1, keepdims=True))
        d_score = (d_capped * (1.0 - jnp.square(capped / SOFT_CAP))).astype(jnp.bfloat16)
        dq_blk = jnp.einsum('bkgqs,bskd->bqkgd', d_score, k_blk, preferred_element_type=jnp.float32)
        dk_blk = jnp.einsum('bkgqs,bqkgd->bskd', d_score, q_blk, preferred_element_type=jnp.float32)
        d_q = lax.dynamic_update_slice_in_dim(d_q, dq_blk, q_start, axis=1)
        d_k = lax.dynamic_update_slice_in_dim(d_k, lax.dynamic_slice_in_dim(d_k, k_start, slab_len, axis=1) + dk_blk, k_start, axis=1)
        d_v = lax.dynamic_update_slice_in_dim(d_v, lax.dynamic_slice_in_dim(d_v, k_start, slab_len, axis=1) + dv_blk, k_start, axis=1)
        return d_q, d_k, d_v

    zero_init = (jnp.zeros(q_all.shape, jnp.float32), jnp.zeros(k_all.shape, jnp.float32), jnp.zeros(v_all.shape, jnp.float32))
    return lax.fori_loop(0, seq_len // q_block, block_step, zero_init)


def solution(mesh):
    act_spec = P('dp', 'tp', None)
    head_spec = P(None, 'tp', None)
    grad_spec = P('dp', 'tp', None)
    in_specs = (act_spec, P('dp', 'tp'), act_spec, head_spec, head_spec, head_spec, P('tp', None, None), P(None), P(None))
    out_specs = (act_spec, act_spec, grad_spec, grad_spec, grad_spec, P(('dp', 'tp'), None, None), P('dp'), P('dp'))

    def local_step(x_in, positions, grad_out, w_query, w_key, w_value, w_out, gain_pre, gain_post):
        heads_loc, head_dim = w_query.shape[1], w_query.shape[2]
        kv_loc = w_key.shape[1]
        groups = heads_loc // kv_loc
        q_scale = head_dim ** -0.5
        normed, pre_pullback = jax.vjp(rms_norm, x_in, gain_pre)
        normed_all = lax.all_gather(normed, 'tp', axis=1, tiled=True)
        pos_all = lax.all_gather(positions, 'tp', axis=1, tiled=True)
        n_rows, seq_len = pos_all.shape
        cos_t, sin_t = rope_tables(pos_all, head_dim)
        q_lin = jnp.einsum('bsd,dhe->bshe', normed_all, w_query, preferred_element_type=jnp.float32)
        k_lin = jnp.einsum('bsd,dhe->bshe', normed_all, w_key, preferred_element_type=jnp.float32)
        v_lin = jnp.einsum('bsd,dhe->bshe', normed_all, w_value, preferred_element_type=jnp.float32)
        q_all = (apply_rope(q_lin, cos_t, sin_t) * q_scale).astype(jnp.bfloat16).reshape(n_rows, seq_len, kv_loc, groups, head_dim)
        k_all = apply_rope(k_lin, cos_t, sin_t).astype(jnp.bfloat16)
        v_all = v_lin.astype(jnp.bfloat16)
        attn_out = attention_fwd(q_all, k_all, v_all, pos_all).reshape(n_rows, seq_len, heads_loc, head_dim)
        part_proj = jnp.einsum('bshe,hed->bsd', attn_out, w_out, preferred_element_type=jnp.float32)
        proj_loc = lax.psum_scatter(part_proj.astype(jnp.bfloat16), 'tp', scatter_dimension=1, tiled=True)
        post_norm, post_pullback = jax.vjp(rms_norm, proj_loc, gain_post)
        y_out = (x_in.astype(jnp.float32) + post_norm.astype(jnp.float32)).astype(jnp.bfloat16)
        d_proj, d_gain_post = post_pullback(grad_out)
        d_proj_all = lax.all_gather(d_proj, 'tp', axis=1, tiled=True)
        d_attn = jnp.einsum('bsd,hed->bshe', d_proj_all, w_out, preferred_element_type=jnp.float32).astype(jnp.bfloat16)
        grad_wo = jnp.einsum('bshe,bsd->hed', attn_out, d_proj_all, preferred_element_type=jnp.float32)
        d_q, d_k, d_v = attention_bwd(q_all, k_all, v_all, pos_all, d_attn.reshape(n_rows, seq_len, kv_loc, groups, head_dim))
        dq_lin = (rope_transpose(d_q.reshape(n_rows, seq_len, heads_loc, head_dim), cos_t, sin_t) * q_scale).astype(jnp.bfloat16)
        dk_lin = rope_transpose(d_k, cos_t, sin_t).astype(jnp.bfloat16)
        dv_lin = d_v.astype(jnp.bfloat16)
        grad_wq = jnp.einsum('bsd,bshe->dhe', normed_all, dq_lin, preferred_element_type=jnp.float32)
        grad_wk = jnp.einsum('bsd,bshe->dhe', normed_all, dk_lin, preferred_element_type=jnp.float32)
        grad_wv = jnp.einsum('bsd,bshe->dhe', normed_all, dv_lin, preferred_element_type=jnp.float32)
        d_normed = (jnp.einsum('bshe,dhe->bsd', dq_lin, w_query, preferred_element_type=jnp.float32)
                    + jnp.einsum('bshe,dhe->bsd', dk_lin, w_key, preferred_element_type=jnp.float32)
                    + jnp.einsum('bshe,dhe->bsd', dv_lin, w_value, preferred_element_type=jnp.float32))
        d_normed_loc = lax.psum_scatter(d_normed.astype(jnp.bfloat16), 'tp', scatter_dimension=1, tiled=True)
        d_x_norm, d_gain_pre = pre_pullback(d_normed_loc)
        grad_x = (grad_out.astype(jnp.float32) + d_x_norm.astype(jnp.float32)).astype(jnp.bfloat16)
        grad_pre = lax.psum(d_gain_pre, 'tp')
        grad_post = lax.psum(d_gain_post, 'tp')
        return y_out, grad_x, grad_wq, grad_wk, grad_wv, grad_wo, grad_pre, grad_post

    return jax.shard_map(local_step, mesh=mesh, in_specs=in_specs, out_specs=out_specs, check_vma=False)
```

profile of v0, /device:TPU:89, one launch (start us, length us, event | category | flops | bytes accessed | tf_op | source)
XLA Modules:
  0.0 1449.1 jit_solution(8034885129151535056)
XLA Ops:
  14.5 13.9 all_gather.9
  35.8 92.9 %all-gather.3.cloned.1.call-done = bf16[1,3072,3840]{2,1,0:T(8,128)(2,1)} async-done(((bf16[1,384,3840]{2,1,0:T(8,128)(2,1)}), bf16[1,3072,3840]{2,1,0:T(8,128)(2,1)}) %all-gather.3.cloned.1.call-update) | async-done | bytes 23592976 | tf_op jit(solution)/shard_map/all_gather | solution.py:111
  128.7 12.7 fusion.113
  141.4 8.3 fusion.144
  153.4 18.6 %fusion.107 = f32[1,3072,2,256]{1,3,2,0:T(8,128)} fusion(bf16[1,3072,3840]{2,1,0:T(8,128)(2,1)} %all-gather.3.cloned.1.call-done, bf16[3840,2,256]{2,1,0:T(2,128)(2,1)} %param.16), kind=kOutput, calls=%fused_computation.126 | convolution fusion | flops 12079595520 | bytes 33816576 | tf_op jit(solution)/shard_map/bsd,dhe->bshe/dot_general | solution.py:115
  182.9 12.7 fusion.122
  197.5 154.2 %while.33 = (s32[]{:T(128)}, bf16[1,3072,1,2,256]{4,1,3,2,0:T(8,128)(2,1)}, s32[1,3072]{1,0:T(1,128)S(1)}, bf16[1,3072,1,2,256]{4,1,3,2,0:T(8,128)(2,1)}, bf16[1...) while((s32[]{:T(128)}, ...), condition=%wide.region_4.5_spmd, body=%wide.region_1.4_spmd.sunk | while | flops 814022144 | bytes 13650591 | solution.py:64
  351.7 19.5 %fusion.82 = bf16[1,3072,3840]{2,1,0:T(8,128)(2,1)} fusion(bf16[2,256,3840]{2,1,0:T(8,128)(2,1)} %param.19, bf16[1,3072,1,2,256]{4,1,3,2,0:T(8,128)(2,1)} %get-tuple-element.339), kind=kOutput, calls=%fused_computation.87 | convolution fusion | flops 12091392000 | bytes 30670848 | tf_op jit(solution)/shard_map/bshe,hed->bsd/dot_general | solution.py:122
  371.9 120.3 %reduce-scatter.3.cloned.1.call-done = bf16[1,384,3840]{2,1,0:T(8,128)(2,1)} async-done(((bf16[1,3072,3840]{2,1,0:T(8,128)(2,1)}), bf16[1,384,3840]{2,1,0:T(8,128)(2,1)}) %reduce-scatter.3.cloned.1.call-update) | async-done | bytes 2949136 | tf_op jit(solution)/shard_map/reduce_scatter | solution.py:123
  505.8 111.5 %all-gather.5.cloned.1.call-done = bf16[1,3072,3840]{2,1,0:T(8,128)(2,1)} async-done(((bf16[1,384,3840]{2,1,0:T(8,128)(2,1)}), bf16[1,3072,3840]{2,1,0:T(8,128)(2,1)}) %all-gather.5.cloned.1.call-update) | async-done | bytes 23592976 | tf_op jit(solution)/shard_map/all_gather | solution.py:127
  617.3 19.3 %fusion.116 = bf16[1,3072,1,2,256]{4,1,3,2,0:T(8,128)(2,1)} fusion(bf16[2,256,3840]{2,1,0:T(8,128)(2,1)} %param.19, bf16[1,3072,3840]{2,1,0:T(8,128)(2,1)} %all-gather.5.cloned.1.call-done), kind=kOutput, calls=%fused_computation.129 | convolution fusion | flops 12081168384 | bytes 30670848 | tf_op jit(solution)/shard_map/bsd,hed->bshe/dot_general | solution.py:128
  640.1 549.8 %while.34 = (s32[]{:T(128)}, f32[1,3072,1,2,256]{1,4,3,2,0:T(8,128)}, f32[1,3072,1,256]{1,3,2,0:T(8,128)}, f32[1,3072,1,256]{1,3,2,0:T(8,128)}, s32[1,3072]{1,0:...) while((s32[]{:T(128)}, ...), condition=%wide.region_12.0_spmd.clone, body=%wide.region_8.12_spmd.clone.sunk | while | flops 2040790272 | bytes 49308400 | solution.py:95
  1189.9 8.1 add_bitcast_fusion
  1204.2 19.1 %fusion.137 = f32[3072,3840]{1,0:T(8,128)} fusion(bf16[3840,1,256]{2,0,1:T(8,128)(2,1)S(1)} %copy-done, f32[1,3072,1,256]{1,3,2,0:T(8,128)} %get-tuple-element.342), kind=kOutput, calls=%fused_computation.152 | convolution fusion | flops 6040584192 | bytes 52297728 | tf_op jit(solution)/shard_map/bshe,dhe->bsd/dot_general | solution.py:139
  1223.3 19.8 %fusion.140 = f32[3072,3840]{1,0:T(8,128)} fusion(bf16[3840,1,256]{2,0,1:T(8,128)(2,1)} %param.17, bf16[3072,128]{0,1:T(8,128)(2,1)S(1)} %get-tuple-element.443, bf16[3072,128]{0,1:T(8,128)(2,1)S(1)} %get-tuple-element.442), kind=kOutput, calls=%fused_computation.155 | convolution fusion | flops 6042943488 | bytes 50724864 | tf_op jit(solution)/shard_map/bshe,dhe->bsd/dot_general | solution.py:138
  1243.0 42.2 %fusion.81 = bf16[1,3072,3840]{2,1,0:T(8,128)(2,1)} fusion(f32[3072,3840]{1,0:T(8,128)} %fusion.137, f32[3072,3840]{1,0:T(8,128)} %fusion.140, bf16[3840,2,256]{2,1,0:T(2,128)(2,1)} %param.16, f32[3072,2,128]{0,2,1:T(8,128)} %get-tuple-element.439, f32[3072,2,128]{0,2,1:T(8,128)} %get-tuple-element.438), kind=kOutput, calls=%fused_computation.86 | convolution fusion | flops 12119703552 | bytes 128188416 | tf_op jit(solution)/shard_map/bshe,dhe->bsd/dot_general | solution.py:137
  1285.3 11.8 fusion.104
  1297.1 18.1 %copy.31 = f32[3840,1,256]{2,1,0:T(1,128)} copy(f32[3840,1,256]{2,0,1:T(8,128)S(1)} %fusion.104) | data formatting | bytes 7864320
  1315.2 20.2 %fusion.69 = f32[3840,2,256]{2,0,1:T(8,128)} fusion(bf16[1,3072,3840]{2,1,0:T(8,128)(2,1)} %all-gather.3.cloned.1.call-done, f32[3072,2,128]{0,2,1:T(8,128)} %get-tuple-element.439, f32[3072,2,128]{0,2,1:T(8,128)S(1)} %copy-done.9), kind=kOutput, calls=%fused_computation.74 | convolution fusion | flops 12084314112 | bytes 37748736 | tf_op jit(solution)/shard_map/bsd,bshe->dhe/dot_general | solution.py:134
  1335.4 23.5 %copy.30 = f32[3840,2,256]{2,1,0:T(2,128)} copy(f32[3840,2,256]{2,0,1:T(8,128)} %fusion.69) | data formatting | bytes 15728640
  1359.0 12.5 fusion.101
  1371.5 18.1 %copy.32 = f32[3840,1,256]{2,1,0:T(1,128)} copy(f32[3840,1,256]{2,0,1:T(8,128)S(1)} %fusion.101) | data formatting | bytes 7864320
  1389.6 18.3 %fusion.65 = f32[2,256,3840]{2,1,0:T(8,128)} fusion(bf16[1,3072,3840]{2,1,0:T(8,128)(2,1)} %all-gather.5.cloned.1.call-done, bf16[1,3072,1,2,256]{4,1,3,2,0:T(8,128)(2,1)S(1)} %copy-done.10), kind=kOutput, calls=%fused_computation.70 | convolution fusion | flops 12079595520 | bytes 34603008 | tf_op jit(solution)/shard_map/bshe,bsd->hed/dot_general | solution.py:129
  1414.3 22.3 %all-reduce = (f32[3840]{0:T(1024)}, f32[3840]{0:T(1024)}) all-reduce(f32[3840]{0:T(1024)S(1)} %get-tuple-element.398, f32[3840]{0:T(1024)S(1)} %copy-done.15), channel_id=1, replica_groups=mesh['dp'=4,'tp'=8] {'tp'}, use_global_device_ids=true, to_apply=%region_16.17 | all-reduce | flops 7680 | bytes 61440 | tf_op jit(solution)/shard_map/psum | solution.py:143
  (513 shorter events, 770.2 us)
Async XLA Ops:
  7.2 175.7 %copy-start = (bf16[3840,1,256]{2,0,1:T(8,128)(2,1)S(1)}, bf16[3840,1,256]{2,0,1:T(8,128)(2,1)}, u32[]{:S(2)}) copy-start(bf16[3840,1,256]{2,0,1:T(8,128)(2,1)} %param.18) | copy-start | bytes 5898244
  7.2 121.5 %all-gather.3.cloned.1.call-start = ((), (), s32[]{:S(2)}) async-start(), calls=%async_computation.2 | async-start | bytes 26542080 | tf_op jit(solution)/shard_map/all_gather | solution.py:111
  7.3 4.6 copy-start.2
  14.4 477.8 %reduce-scatter.3.cloned.1.call-start = ((), (), s32[]{:S(2)}) async-start(), calls=%async_computation.3 | async-start | bytes 26542080 | tf_op jit(solution)/shard_map/reduce_scatter | solution.py:123
  28.5 112.9 %copy-start.21 = (f32[128]{0:T(128)}, f32[128]{0:T(128)S(1)}, u32[]{:S(2)}) copy-start(f32[128]{0:T(128)S(1)} %multiply_power_fusion) | copy-start | bytes 1540
  35.8 136.2 %copy-start.7 = (f32[3072,128]{0,1:T(8,128)}, f32[3072,128]{0,1:T(8,128)S(1)}, u32[]{:S(2)}) copy-start(f32[3072,128]{0,1:T(8,128)S(1)} %get-tuple-element.448) | copy-start | bytes 4718596
  153.4 18.6 %copy-start.8 = (f32[3072,128]{0,1:T(8,128)S(1)}, f32[3072,128]{0,1:T(8,128)}, u32[]{:S(2)}) copy-start(f32[3072,128]{0,1:T(8,128)} %get-tuple-element.449) | copy-start | bytes 4718596
  371.2 246.1 %all-gather.5.cloned.1.call-start = ((), (), s32[]{:S(2)}) async-start(), calls=%async_computation.4 | async-start | bytes 26542080 | tf_op jit(solution)/shard_map/all_gather | solution.py:127
  494.9 6.2 copy-start.3
  494.9 6.2 copy-start.5
  505.6 902.4 %reduce-scatter.5.cloned.1.call-start = ((), (), s32[]{:S(2)}) async-start(), calls=%async_computation.5 | async-start | bytes 26542080 | tf_op jit(solution)/shard_map/reduce_scatter | solution.py:140
  678.9 4.3 copy-start.6
  724.9 4.3 copy-start.6
  747.9 4.3 copy-start.6
  793.9 4.3 copy-start.6
  1189.9 8.1 copy-start.1
  1189.9 8.1 copy-start.14
  1189.9 8.1 copy-start.22
  1297.1 18.1 %copy-start.9 = (f32[3072,2,128]{0,2,1:T(8,128)S(1)}, f32[3072,2,128]{0,2,1:T(8,128)}, u32[]{:S(2)}) copy-start(f32[3072,2,128]{0,2,1:T(8,128)} %get-tuple-element.438) | copy-start | bytes 9437188
  1371.5 18.1 %copy-start.10 = (bf16[1,3072,1,2,256]{4,1,3,2,0:T(8,128)(2,1)S(1)}, bf16[1,3072,1,2,256]{4,1,3,2,0:T(8,128)(2,1)}, u32[]{:S(2)}) copy-start(bf16[1,3072,1,2,256]{4,1,3,2,0:T(8,128)(2,1)} %get-tuple-element.339) | copy-start | bytes 9437188
  1389.6 18.4 %copy-start.12 = (f32[3840]{0:T(1024)S(1)}, f32[3840]{0:T(1024)}, u32[]{:S(2)}) copy-start(f32[3840]{0:T(1024)} %copy-done.11) | copy-start | bytes 46084
  1389.6 18.4 %copy-start.17 = (f32[384]{0:T(512)S(1)}, f32[384]{0:T(512)}, u32[]{:S(2)}) copy-start(f32[384]{0:T(512)} %copy-done.16) | copy-start | bytes 4612
  1407.9 6.4 copy-start.19
  1407.9 6.4 copy-start.15
  (27 other events, 93.2 us)
Sparse Core Ops, SparseCore 0:
  14.5 114.1 all-gather.2
  371.4 120.8 reduce-scatter.2
  505.7 111.5 all-gather.4
  1285.4 120.8 reduce-scatter.4
where the time goes:
time: 1460 us; the launch traced here: 1450 us
  matrix products  778 us (53%)
  waiting for transfers between devices  325 us (22%)
  other arithmetic  159 us (11%)
  local copies, waits for them, and re-layouts  135 us (9%)
  blocking collectives  36.2 us (2%)
    dot_general x48, matrix products, block_probs(): jnp.einsum('bqkgd,bskd->bkgqs', q_blk, k_blk, preferred_element_type=jnp....  126 us
    dot_general x24, matrix products, block_step(): jnp.einsum('bkgqs,bqkgd->bskd', prob_blk.astype(jnp.bfloat16), do_blk, pr...  122 us
    reduce_scatter x1, waiting for transfers between devices, local_step(): lax.psum_scatter(part_proj.astype(jnp.bfloat16), 'tp', scatter_dimension=...  120 us
    all_gather x1, waiting for transfers between devices, local_step(): d_proj_all = lax.all_gather(d_proj, 'tp', axis=1, tiled=True)  111 us
    dot_general x24, matrix products, block_step(): jnp.einsum('bkgqs,bqkgd->bskd', d_score, q_blk, preferred_element_type=jn...  102 us
    all_gather x1, waiting for transfers between devices, local_step(): normed_all = lax.all_gather(normed, 'tp', axis=1, tiled=True)  92.9 us
    dot_general x24, matrix products, block_step(): jnp.einsum('bqkgd,bskd->bkgqs', do_blk, v_blk, preferred_element_type=jnp...  69.9 us
    dot_general x24, matrix products, block_step(): jnp.einsum('bkgqs,bskd->bqkgd', prob_blk.astype(jnp.bfloat16), v_blk, pre...  67.3 us
  transfers between devices with their start and end apart: 4, of which 3 were waited for; matrix products, arithmetic and copies ran while one was open for 9% of the time, Pallas kernels for 0%

commit v1 on v0

v1 whole, which is shorter than its diff:
```python
import functools

import jax
import jax.numpy as jnp
from jax import lax
from jax.experimental import pallas as pl
from jax.experimental.pallas import tpu as pltpu
from jax.sharding import PartitionSpec as P

WINDOW = 4096
SOFT_CAP = 50.0
NORM_EPS = 1e-6
ROPE_THETA = 10000.0
ROWS = 128
LOG2E = 1.4426950408889634
VMEM_LIMIT = 60 * 1024 * 1024


def rms_norm(hidden, scale_w):
    values = hidden.astype(jnp.float32)
    inv_rms = lax.rsqrt(jnp.mean(values * values, axis=-1, keepdims=True) + NORM_EPS)
    return (values * inv_rms * (1.0 + scale_w)).astype(jnp.bfloat16)


def params(n=1):
    return pltpu.CompilerParams(dimension_semantics=("arbitrary",) * n, vmem_limit_bytes=VMEM_LIMIT)


def qkv_kernel(n_heads, scale, a_ref, w_ref, cos_ref, sin_ref, q_ref, k_ref, kt_ref, v_ref, vt_ref):
    owners, n_chunks, _, d_model = a_ref.shape
    rows2 = owners * n_chunks * ROWS
    rows = n_chunks * ROWS
    lin = jnp.dot(a_ref[...].reshape(rows2, d_model), w_ref[...], preferred_element_type=jnp.float32)
    half = cos_ref.shape[-1]
    hd = 2 * half
    cos = cos_ref[...].reshape(rows2, half)
    sin = sin_ref[...].reshape(rows2, half)

    def rope(col):
        lo = lin[:, col:col + half]
        hi = lin[:, col + half:col + hd]
        return lo * cos - hi * sin, hi * cos + lo * sin

    for h in range(n_heads):
        lo, hi = rope(h * hd)
        q_ref[..., h * hd:h * hd + half] = (lo * scale).astype(jnp.bfloat16).reshape(owners, n_chunks, ROWS, half)
        q_ref[..., h * hd + half:(h + 1) * hd] = (hi * scale).astype(jnp.bfloat16).reshape(owners, n_chunks, ROWS, half)
    lo, hi = rope(n_heads * hd)
    k = jnp.concatenate([lo.astype(jnp.bfloat16), hi.astype(jnp.bfloat16)], axis=1)
    v = lin[:, (n_heads + 1) * hd:].astype(jnp.bfloat16)
    for i in range(owners):
        for c in range(n_chunks):
            at = i * rows + c * ROWS
            k_i = k[at:at + ROWS]
            v_i = v[at:at + ROWS]
            k_ref[i, c] = k_i
            kt_ref[i, c] = k_i.T
            v_ref[i, c] = v_i
            vt_ref[i, c] = v_i.T


def qkv(n_heads, scale, a, w, cos_t, sin_t):
    n_own, n_chunks, rows, d_model = a.shape
    hd = 2 * cos_t.shape[-1]
    bf = lambda s: jax.ShapeDtypeStruct((n_own, n_chunks) + s, jnp.bfloat16)
    blk = lambda s: pl.BlockSpec((1, n_chunks) + s, lambda i: (i, 0, 0, 0))
    outs = [(rows, n_heads * hd), (rows, hd), (hd, rows), (rows, hd), (hd, rows)]
    return pl.pallas_call(
        functools.partial(qkv_kernel, n_heads, scale),
        grid=(n_own,),
        in_specs=[blk((rows, d_model)), pl.BlockSpec(w.shape, lambda i: (0, 0)), blk((rows, hd // 2)), blk((rows, hd // 2))],
        out_specs=[blk(o) for o in outs],
        out_shape=[bf(o) for o in outs],
        compiler_params=params(),
        cost_estimate=pl.CostEstimate(flops=2 * a.size * w.shape[1], transcendentals=0, bytes_accessed=2 * (a.size + w.size)),
        name="qkv_rope",
    )(a, w, cos_t, sin_t)


def key_mask(posq_ref, posk_ref, blk):
    gap = posq_ref[0] - posk_ref[blk]
    return (gap >= 0) & (gap < WINDOW)


def masked_exp(t, mask, n_heads):
    e = jnp.exp2(t * (SOFT_CAP * LOG2E))
    return jnp.concatenate([jnp.where(mask, e[:, h * ROWS:(h + 1) * ROWS], 0.0) for h in range(n_heads)], axis=1)


def fwd_kernel(n_heads, lo_ref, q_ref, k_ref, vt_ref, posq_ref, posk_ref, o_ref, ot_ref, qt_ref, li_ref, acc_ref):
    own = pl.program_id(0)
    n_chunks, hd = k_ref.shape[1], k_ref.shape[3]
    q = q_ref[0, 0]
    qt = jnp.concatenate([q[:, h * hd:(h + 1) * hd].T for h in range(n_heads)], axis=1)
    qt_ref[0] = qt
    acc_ref[...] = jnp.zeros_like(acc_ref)

    def body(blk, l_sum):
        k_b = k_ref[blk].reshape(n_chunks * ROWS, hd)
        s = jnp.dot(k_b, qt_ref[0], preferred_element_type=jnp.float32)
        t = jnp.tanh(s * (1.0 / SOFT_CAP))
        e = masked_exp(t, key_mask(posq_ref, posk_ref, blk), n_heads)
        vt = jnp.concatenate([vt_ref[blk, c] for c in range(n_chunks)], axis=1)
        acc_ref[...] += jnp.dot(vt, e.astype(jnp.bfloat16), preferred_element_type=jnp.float32)
        return l_sum + jnp.sum(e, axis=0, keepdims=True)

    l_sum = lax.fori_loop(lo_ref[own], own + 1, body, jnp.zeros((1, n_heads * ROWS), jnp.float32))
    inv = 1.0 / l_sum
    li_ref[0] = inv
    ot = (acc_ref[...] * inv).astype(jnp.bfloat16)
    ot_ref[0] = ot
    for h in range(n_heads):
        o_ref[0, :, h * hd:(h + 1) * hd] = ot[:, h * ROWS:(h + 1) * ROWS].T


def attn_fwd(n_heads, chunk, lo, q, k, vt, posq, posk):
    n_own, n_chunks, rows, hd = k.shape
    lanes = n_heads * rows
    full = lambda x: pl.BlockSpec(x.shape, lambda i, lo: (0,) * x.ndim)
    per = lambda s: pl.BlockSpec((1,) + s, lambda i, lo: (i, 0, 0))
    return pl.pallas_call(
        functools.partial(fwd_kernel, n_heads),
        grid_spec=pltpu.PrefetchScalarGridSpec(
            num_scalar_prefetch=1, grid=(n_own,),
            in_specs=[pl.BlockSpec((1, 1, rows, n_heads * hd), lambda i, lo: (i, chunk, 0, 0)), full(k), full(vt), per((1, rows)), full(posk)],
            out_specs=[per((rows, n_heads * hd)), per((hd, lanes)), per((hd, lanes)), per((1, lanes))],
            scratch_shapes=[pltpu.VMEM((hd, lanes), jnp.float32)]),
        out_shape=[jax.ShapeDtypeStruct((n_own, rows, n_heads * hd), jnp.bfloat16),
                   jax.ShapeDtypeStruct((n_own, hd, lanes), jnp.bfloat16),
                   jax.ShapeDtypeStruct((n_own, hd, lanes), jnp.bfloat16),
                   jax.ShapeDtypeStruct((n_own, 1, lanes), jnp.float32)],
        compiler_params=params(),
        cost_estimate=pl.CostEstimate(flops=4 * n_own * lanes * (n_own * n_chunks * rows // 2) * hd,
                                      transcendentals=0, bytes_accessed=12 * k.size),
        name="attn_fwd",
    )(lo, q, k, vt, posq, posk)


def bwd_kernel(n_heads, scale, chunk, first, last, *refs):
    lo_ref, q_ref, qt_ref, ot_ref, li_ref, do_ref, k_ref, kt_ref, v_ref, posq_ref, posk_ref, cos_ref, sin_ref = refs[:13]
    rest = refs[13:]
    if not first:
        dki_ref, dvi_ref = rest[:2]
        rest = rest[2:]
    dq_ref, dk_out, dv_out = rest[:3]
    if last:
        dk_ref, dv_ref = rest[3:5]
        rest = rest[5:]
    else:
        dk_ref, dv_ref = dk_out, dv_out
        rest = rest[3:]
    dqt_ref, dot_ref, dos_ref, qs_ref = rest
    own = pl.program_id(0)
    n_own, n_chunks, _, hd = k_ref.shape
    half = hd // 2

    @pl.when(own == 0)
    def _():
        if first:
            dk_ref[...] = jnp.zeros_like(dk_ref)
            dv_ref[...] = jnp.zeros_like(dv_ref)
        else:
            dk_ref[...] = dki_ref[...]
            dv_ref[...] = dvi_ref[...]

    do = do_ref[0]
    q = q_ref[0, 0]
    for h in range(n_heads):
        dos_ref[h * ROWS:(h + 1) * ROWS] = do[:, h * hd:(h + 1) * hd]
        qs_ref[h * ROWS:(h + 1) * ROWS] = q[:, h * hd:(h + 1) * hd]
        dot_ref[:, h * ROWS:(h + 1) * ROWS] = do[:, h * hd:(h + 1) * hd].T
    delta = jnp.sum(dot_ref[...].astype(jnp.float32) * ot_ref[0].astype(jnp.float32), axis=0, keepdims=True)
    inv = li_ref[0]
    dqt_ref[...] = jnp.zeros_like(dqt_ref)

    def body(blk, carry):
        k_b = k_ref[blk].reshape(n_chunks * ROWS, hd)
        v_b = v_ref[blk].reshape(n_chunks * ROWS, hd)
        s = jnp.dot(k_b, qt_ref[0], preferred_element_type=jnp.float32)
        dp = jnp.dot(v_b, dot_ref[...], preferred_element_type=jnp.float32)
        t = jnp.tanh(s * (1.0 / SOFT_CAP))
        p = masked_exp(t, key_mask(posq_ref, posk_ref, blk), n_heads) * inv
        ds = (p * (dp - delta) * (1.0 - t * t)).astype(jnp.bfloat16)
        dv_ref[blk] += jnp.dot(p.astype(jnp.bfloat16), dos_ref[...], preferred_element_type=jnp.float32)
        dk_ref[blk] += jnp.dot(ds, qs_ref[...], preferred_element_type=jnp.float32)
        kt = jnp.concatenate([kt_ref[blk, c] for c in range(n_chunks)], axis=1)
        dqt_ref[...] += jnp.dot(kt, ds, preferred_element_type=jnp.float32)
        return carry

    lax.fori_loop(lo_ref[own], own + 1, body, 0)

    def unrope(grad, cos, sin):
        lo, hi = grad[:, :half], grad[:, half:]
        return lo * cos + hi * sin, hi * cos - lo * sin

    cos, sin = cos_ref[own, chunk], sin_ref[own, chunk]
    for h in range(n_heads):
        lo, hi = unrope(dqt_ref[:, h * ROWS:(h + 1) * ROWS].T, cos, sin)
        dq_ref[0, :, h * hd:h * hd + half] = (lo * scale).astype(jnp.bfloat16)
        dq_ref[0, :, h * hd + half:(h + 1) * hd] = (hi * scale).astype(jnp.bfloat16)

    if last:
        @pl.when(own == n_own - 1)
        def _():
            def fin(i, carry):
                for c in range(n_chunks):
                    lo, hi = unrope(dk_ref[i, c * ROWS:(c + 1) * ROWS], cos_ref[i, c], sin_ref[i, c])
                    dk_out[i, c, :, :half] = lo.astype(jnp.bfloat16)
                    dk_out[i, c, :, half:] = hi.astype(jnp.bfloat16)
                    dv_out[i, c] = dv_ref[i, c * ROWS:(c + 1) * ROWS].astype(jnp.bfloat16)
                return carry
            lax.fori_loop(0, n_own, fin, 0)


def attn_bwd(n_heads, scale, chunk, first, last, lo, q, qt, ot, li, do, k, kt, v, posq, posk, cos_t, sin_t, prev):
    n_own, n_chunks, rows, hd = k.shape
    lanes = n_heads * rows
    full = lambda x: pl.BlockSpec(x.shape, lambda i, lo: (0,) * x.ndim)
    per = lambda s: pl.BlockSpec((1,) + s, lambda i, lo: (i, 0, 0))
    acc = jax.ShapeDtypeStruct((n_own, n_chunks * rows, hd), jnp.float32)
    fin = jax.ShapeDtypeStruct((n_own, n_chunks, rows, hd), jnp.bfloat16)
    kv_out = fin if last else acc
    scratch = [pltpu.VMEM(acc.shape, jnp.float32)] * 2 if last else []
    scratch += [pltpu.VMEM((hd, lanes), jnp.float32), pltpu.VMEM((hd, lanes), jnp.bfloat16),
                pltpu.VMEM((lanes, hd), jnp.bfloat16), pltpu.VMEM((lanes, hd), jnp.bfloat16)]
    return pl.pallas_call(
        functools.partial(bwd_kernel, n_heads, scale, chunk, first, last),
        grid_spec=pltpu.PrefetchScalarGridSpec(
            num_scalar_prefetch=1, grid=(n_own,),
            in_specs=[pl.BlockSpec((1, 1, rows, n_heads * hd), lambda i, lo: (i, chunk, 0, 0)), per((hd, lanes)), per((hd, lanes)), per((1, lanes)),
                      per((rows, n_heads * hd)), full(k), full(kt), full(v), per((1, rows)), full(posk),
                      full(cos_t), full(sin_t)] + [full(x) for x in prev],
            out_specs=[per((rows, n_heads * hd)), full(kv_out), full(kv_out)],
            scratch_shapes=scratch),
        out_shape=[jax.ShapeDtypeStruct((n_own, rows, n_heads * hd), jnp.bfloat16), kv_out, kv_out],
        compiler_params=params(),
        cost_estimate=pl.CostEstimate(flops=10 * n_own * lanes * (n_own * n_chunks * rows // 2) * hd,
                                      transcendentals=0, bytes_accessed=24 * k.size),
        name="attn_bwd",
    )(lo, q, qt, ot, li, do, k, kt, v, posq, posk, cos_t, sin_t, *prev)


def matmul(lhs, rhs, dims):
    return lax.dot_general(lhs, rhs, (dims, ((), ())), preferred_element_type=jnp.float32)


def solution(mesh):
    act_spec = P('dp', 'tp', None)
    head_spec = P(None, 'tp', None)
    grad_spec = P('dp', 'tp', None)
    in_specs = (act_spec, P('dp', 'tp'), act_spec, head_spec, head_spec, head_spec, P('tp', None, None), P(None), P(None))
    out_specs = (act_spec, act_spec, grad_spec, grad_spec, grad_spec, P(('dp', 'tp'), None, None), P('dp'), P('dp'))
    n_own = mesh.shape['tp']

    def local_step(x_in, positions, grad_out, w_query, w_key, w_value, w_out, gain_pre, gain_post):
        d_model, n_heads, hd = w_query.shape
        loc = x_in.shape[1]
        n_chunks = loc // ROWS
        scale = hd ** -0.5
        half = hd // 2
        qw = n_heads * hd
        chunks = range(n_chunks)
        x_c = [x_in[0, c * ROWS:(c + 1) * ROWS] for c in chunks]
        g_c = [grad_out[0, c * ROWS:(c + 1) * ROWS] for c in chunks]
        w_cat = jnp.concatenate([w_query.reshape(d_model, qw), w_key.reshape(d_model, hd), w_value.reshape(d_model, hd)], axis=1)
        wo = w_out.reshape(qw, d_model)

        normed, pre_pullback = jax.vjp(rms_norm, x_in[0], gain_pre)
        a_all = lax.all_gather(normed, 'tp', axis=0, tiled=True)
        pos = lax.all_gather(positions, 'tp', axis=1, tiled=True).reshape(n_own, n_chunks, ROWS)
        inv_freq = ROPE_THETA ** (-2.0 * jnp.arange(half, dtype=jnp.float32) / hd)
        angles = pos.astype(jnp.float32)[..., None] * inv_freq
        cos_t, sin_t = jnp.cos(angles), jnp.sin(angles)
        pos_k = jnp.broadcast_to(pos.reshape(n_own, loc, 1), (n_own, loc, ROWS))
        k_last = pos[:, -1, -1]
        lo = jnp.sum((pos[:, :, :1] - k_last >= WINDOW).astype(jnp.int32), axis=-1)
        pos_q = [pos[:, c:c + 1] for c in chunks]
        lo_c = [lo[:, c] for c in chunks]

        q_all, k_all, kt_all, v_all, vt_all = qkv(n_heads, scale, a_all.reshape(n_own, n_chunks, ROWS, d_model), w_cat, cos_t, sin_t)

        saved, r_c = [], []
        for c in chunks:
            o, ot, qt, li = attn_fwd(n_heads, c, lo_c[c], q_all, k_all, vt_all, pos_q[c], pos_k)
            saved.append((o, ot, qt, li))
            part = matmul(o.reshape(n_own * ROWS, qw), wo, ((1,), (0,))).astype(jnp.bfloat16)
            r_c.append(lax.psum_scatter(part, 'tp', scatter_dimension=0, tiled=True))

        y_c, dp_c, d_gain_post = [], [], 0.0
        for c in chunks:
            post, pullback = jax.vjp(rms_norm, r_c[c], gain_post)
            y_c.append((x_c[c].astype(jnp.float32) + post.astype(jnp.float32)).astype(jnp.bfloat16))
            d_proj, d_gain = pullback(g_c[c])
            d_gain_post = d_gain_post + d_gain
            dp_c.append(lax.all_gather(d_proj, 'tp', axis=0, tiled=True))

        dq_c, dkv = [], ()
        for c in chunks:
            o, ot, qt, li = saved[c]
            do = matmul(dp_c[c], wo, ((1,), (1,))).astype(jnp.bfloat16).reshape(n_own, ROWS, qw)
            dq, *dkv = attn_bwd(n_heads, scale, c, c == 0, c == n_chunks - 1, lo_c[c], q_all, qt, ot, li, do,
                                k_all, kt_all, v_all, pos_q[c], pos_k, cos_t, sin_t, dkv)
            dq_c.append(dq)
        dk_all, dv_all = dkv

        dcat = jnp.concatenate([jnp.stack(dq_c, axis=1), dk_all, dv_all], axis=-1)
        da_c = []
        for c in chunks:
            part = matmul(dcat[:, c].reshape(n_own * ROWS, qw + 2 * hd), w_cat, ((1,), (1,))).astype(jnp.bfloat16)
            da_c.append(lax.psum_scatter(part, 'tp', scatter_dimension=0, tiled=True))
        grad_wo = sum(matmul(saved[c][0].reshape(n_own * ROWS, qw), dp_c[c], ((0,), (0,))) for c in chunks).reshape(n_heads, hd, d_model)
        g_cat = matmul(a_all, dcat.reshape(n_own * loc, qw + 2 * hd), ((0,), (0,)))
        grad_wq = g_cat[:, :qw].reshape(d_model, n_heads, hd)
        grad_wk = g_cat[:, qw:qw + hd].reshape(d_model, 1, hd)
        grad_wv = g_cat[:, qw + hd:].reshape(d_model, 1, hd)

        d_x, d_gain_pre = pre_pullback(jnp.concatenate(da_c, axis=0))
        grad_x = (grad_out.astype(jnp.float32) + d_x.astype(jnp.float32)).astype(jnp.bfloat16)
        grad_pre = lax.psum(d_gain_pre, 'tp')
        grad_post = lax.psum(d_gain_post, 'tp')
        y_out = jnp.concatenate(y_c, axis=0)[None]
        return y_out, grad_x, grad_wq, grad_wk, grad_wv, grad_wo, grad_pre, grad_post

    return jax.shard_map(local_step, mesh=mesh, in_specs=in_specs, out_specs=out_specs, check_vma=False)
```

time: 1460 us -> 733 us (0.50)
  matrix products: 778 us -> 154 us
  Pallas kernels: 0 us -> 156 us
  other arithmetic: 159 us -> 47.6 us
  waiting for transfers between devices: 325 us -> 249 us
  local copies, waits for them, and re-layouts: 135 us -> 60.6 us
    dot_general x180 -> x13, matrix products: 778 us -> 154 us  [matmul(): lax.dot_general(lhs, rhs, (dims, ((), ())), preferred_element_type=jnp.fl...]
    pallas_call x0 -> x7, Pallas kernels: none -> 156 us  [the longest x3 74.5 us: attn_bwd(): pl.pallas_call(functools.partial(bwd_kernel, n_heads, scale, chunk, first...]
    dynamic_update_slice x48 -> x0, local copies, waits for them, and re-layouts: 60.3 us -> none  [block_step(): d_q = lax.dynamic_update_slice_in_dim(d_q, dq_blk, q_start, axis=1)]
    all_gather x2 -> x4, waiting for transfers between devices: 204 us -> 148 us  [the longest x1 83.1 us: local_step(): a_all = lax.all_gather(normed, 'tp', axis=0, tiled=True)]
    another operation x25 -> x0, other arithmetic: 44.6 us -> none
    reduce_sum x48 -> x1, other arithmetic: 34.7 us -> 0.22 us  [local_step(): lo = jnp.sum((pos[:, :, :1] - k_last >= WINDOW).astype(jnp.int32), axis=-1)]
    unnamed x49 -> x60, local copies, waits for them, and re-layouts: 62.1 us -> 40.3 us
    reduce_scatter x2 -> x6, waiting for transfers between devices: 120 us -> 99.9 us  [the longest x3 88.1 us: local_step(): r_c.append(lax.psum_scatter(part, 'tp', scatter_dimension=0, tiled=True))]
  transfers between devices with their start and end apart: 4 -> 10, of which waited for: 3 -> 7; matrix products, arithmetic and copies ran while one was open for 9% -> 26% of each run, Pallas kernels for 0% -> 12%
where the time goes in v1:
time: 733 us; the launch traced here: 720 us
  waiting for transfers between devices  249 us (34%)
  Pallas kernels  156 us (21%)
  matrix products  154 us (21%)
  local copies, waits for them, and re-layouts  60.6 us (8%)
  other arithmetic  47.6 us (6%)
  blocking collectives  36.2 us (5%)
  between operations  14.7 us (2%)
    dot_general x13, matrix products, matmul(): lax.dot_general(lhs, rhs, (dims, ((), ())), preferred_element_type=jnp.fl...  154 us
    reduce_scatter x3, waiting for transfers between devices, local_step(): r_c.append(lax.psum_scatter(part, 'tp', scatter_dimension=0, tiled=True))  88.1 us
    all_gather x1, waiting for transfers between devices, local_step(): a_all = lax.all_gather(normed, 'tp', axis=0, tiled=True)  83.1 us
    pallas_call x3, Pallas kernels, attn_bwd(): pl.pallas_call(functools.partial(bwd_kernel, n_heads, scale, chunk, first...  74.5 us
    all_gather x3, waiting for transfers between devices, local_step(): dp_c.append(lax.all_gather(d_proj, 'tp', axis=0, tiled=True))  64.8 us
    pallas_call x3, Pallas kernels, attn_fwd(): pl.pallas_call(functools.partial(fwd_kernel, n_heads), grid_spec=pltpu.Pr...  49.6 us
    unnamed x60, local copies, waits for them, and re-layouts  40.3 us
    pallas_call x1, Pallas kernels, qkv(): pl.pallas_call(functools.partial(qkv_kernel, n_heads, scale), grid=(n_own...  32.2 us
  transfers between devices with their start and end apart: 10, of which 7 were waited for; matrix products, arithmetic and copies ran while one was open for 26% of the time, Pallas kernels for 12%

profile of v1, /device:TPU:89, one launch (start us, length us, event | category | flops | bytes accessed | tf_op | source)
XLA Modules:
  0.0 720.2 jit_solution(1971119127067881288)
XLA Ops:
  14.5 13.9 %all_gather.15 = s32[1,3072]{1,0:T(1,128)S(1)} all-gather(s32[1,384]{1,0:T(1,128)S(1)} %copy-done.27), channel_id=1, replica_groups=mesh['dp'=4,'tp'=8] {'tp'}, dimensions={1}, use_global_device_ids=true | all-gather | bytes 13824 | tf_op jit(solution)/shard_map/all_gather | solution.py:270
  45.5 83.1 %all-gather.5.cloned.1.call-done = bf16[3072,3840]{1,0:T(8,128)(2,1)} async-done(((bf16[384,3840]{1,0:T(8,128)(2,1)}), bf16[3072,3840]{1,0:T(8,128)(2,1)}) %all-gather.5.cloned.1.call-update) | async-done | bytes 23592976 | tf_op jit(solution)/shard_map/all_gather | solution.py:269
  128.7 32.2 %qkv_rope.1 = (bf16[8,3,128,512]{3,2,1,0:T(8,128)(2,1)}, bf16[8,3,128,256]{3,2,1,0:T(8,128)(2,1)}, bf16[8,3,256,128]{3,2,1,0:T(8,128)(2,1)}, bf16[8,3,128,256]{3,2,1,0:T(8,128)(2,1)}, bf16[8,3,256,128]{3,2,1,0:T(8,128)(2,1)}) custom-call(bf16[8,3,128,3840]{3,2,1,0:T(8,128)(2,1)} %bitcast.140, bf16[3840,1024]{1,0:T(8,128)(2,1)} %pad_maximum_fusion.w_ref, ...), custom_call_target="tpu_custom_call" | custom-call | flops 24159191040 | bytes 31457280 | tf_op jit(solution)/shard_map/qkv_rope/pallas_call | solution.py:68
  162.3 17.4 %attn_fwd.3 = (bf16[8,128,512]{2,1,0:T(8,128)(2,1)}, bf16[8,256,256]{2,1,0:T(8,128)(2,1)}, bf16[8,256,256]{2,1,0:T(8,128)(2,1)}, f32[8,1,256]{2,1,0:T(1,128)}) custom-call(s32[8]{0:T(128)} %get-tuple-element.117.lo_ref.refs_0_, bf16[8,3,128,512]{3,2,1,0:T(8,128)(2,1)} %get-tuple-element.34.q_ref.refs_1_, ...), custom_call_target="tpu_custom_call" | custom-call | flops 3221225472 | bytes 9437184 | tf_op jit(solution)/shard_map/attn_fwd/pallas_call | solution.py:121
  179.8 9.9 %convolution_convert_fusion.5 = bf16[1024,3840]{1,0:T(8,128)(2,1)} fusion(bf16[1024,512]{1,0:T(8,128)(2,1)} %bitcast.128, bf16[512,3840]{1,0:T(8,128)(2,1)} %bitcast.141), kind=kOutput, calls=%fused_computation.8 | convolution fusion | flops 4030464000 | bytes 12845056 | tf_op jit(solution)/shard_map/dot_general | solution.py:244
  190.3 17.2 %attn_fwd.4 = (bf16[8,128,512]{2,1,0:T(8,128)(2,1)}, bf16[8,256,256]{2,1,0:T(8,128)(2,1)}, bf16[8,256,256]{2,1,0:T(8,128)(2,1)}, f32[8,1,256]{2,1,0:T(1,128)}) custom-call(s32[8]{0:T(128)} %get-tuple-element.119.lo_ref.refs_0_, bf16[8,3,128,512]{3,2,1,0:T(8,128)(2,1)} %get-tuple-element.34.q_ref.refs_1_, ...), custom_call_target="tpu_custom_call" | custom-call | flops 3221225472 | bytes 9437184 | tf_op jit(solution)/shard_map/attn_fwd/pallas_call | solution.py:121
  217.5 14.9 %attn_fwd.5 = (bf16[8,128,512]{2,1,0:T(8,128)(2,1)}, bf16[8,256,256]{2,1,0:T(8,128)(2,1)}, bf16[8,256,256]{2,1,0:T(8,128)(2,1)}, f32[8,1,256]{2,1,0:T(1,128)}) custom-call(s32[8]{0:T(128)} %get-tuple-element.118.lo_ref.refs_0_, bf16[8,3,128,512]{3,2,1,0:T(8,128)(2,1)} %get-tuple-element.34.q_ref.refs_1_, ...), custom_call_target="tpu_custom_call" | custom-call | flops 3221225472 | bytes 9437184 | tf_op jit(solution)/shard_map/attn_fwd/pallas_call | solution.py:121
  232.4 9.9 %convolution_convert_fusion.3 = bf16[1024,3840]{1,0:T(8,128)(2,1)} fusion(bf16[1024,512]{1,0:T(8,128)(2,1)} %bitcast.132, bf16[512,3840]{1,0:T(8,128)(2,1)} %bitcast.143), kind=kOutput, calls=%fused_computation.6 | convolution fusion | flops 4030464000 | bytes 12845056 | tf_op jit(solution)/shard_map/dot_general | solution.py:244
  244.5 40.2 %reduce-scatter.9.cloned.1.call-done = bf16[128,3840]{1,0:T(8,128)(2,1)} async-done(((bf16[1024,3840]{1,0:T(8,128)(2,1)}), bf16[128,3840]{1,0:T(8,128)(2,1)}) %reduce-scatter.9.cloned.1.call-update) | async-done | bytes 983056 | tf_op jit(solution)/shard_map/reduce_scatter | solution.py:287
  286.2 47.9 %reduce-scatter.11.cloned.1.call-done = bf16[128,3840]{1,0:T(8,128)(2,1)} async-done(((bf16[1024,3840]{1,0:T(8,128)(2,1)}), bf16[128,3840]{1,0:T(8,128)(2,1)}) %reduce-scatter.11.cloned.1.call-update) | async-done | bytes 983056 | tf_op jit(solution)/shard_map/reduce_scatter | solution.py:287
  347.9 43.2 %all-gather.7.cloned.1.call-done = bf16[1024,3840]{1,0:T(8,128)(2,1)} async-done(((bf16[128,3840]{1,0:T(8,128)(2,1)}), bf16[1024,3840]{1,0:T(8,128)(2,1)}) %all-gather.7.cloned.1.call-update) | async-done | bytes 7864336 | tf_op jit(solution)/shard_map/all_gather | solution.py:295
  400.6 24.9 %attn_bwd.3 = (bf16[8,128,512]{2,1,0:T(8,128)(2,1)}, f32[8,384,256]{2,1,0:T(8,128)}, f32[8,384,256]{2,1,0:T(8,128)}) custom-call(s32[8]{0:T(128)} %get-tuple-element.117.lo_ref.refs_0_, bf16[8,3,128,512]{3,2,1,0:T(8,128)(2,1)} %get-tuple-element.34.q_ref.refs_1_, bf16[8,256,256]{2,1,0:T(8,128)(2,1)} %get-tuple-element.40.refs_2_, ...), custom_call_target="tpu_custom_call" | custom-call | flops 8053063680 | bytes 18874368 | tf_op jit(solution)/shard_map/attn_bwd/pallas_call | solution.py:226
  425.5 11.4 %all-gather.9.cloned.1.call-done = bf16[1024,3840]{1,0:T(8,128)(2,1)} async-done(((bf16[128,3840]{1,0:T(8,128)(2,1)}), bf16[1024,3840]{1,0:T(8,128)(2,1)}) %all-gather.9.cloned.1.call-update) | async-done | bytes 7864336 | tf_op jit(solution)/shard_map/all_gather | solution.py:295
  446.5 26.2 %attn_bwd.4 = (bf16[8,128,512]{2,1,0:T(8,128)(2,1)}, f32[8,384,256]{2,1,0:T(8,128)}, f32[8,384,256]{2,1,0:T(8,128)}) custom-call(s32[8]{0:T(128)} %get-tuple-element.119.lo_ref.refs_0_, bf16[8,3,128,512]{3,2,1,0:T(8,128)(2,1)} %get-tuple-element.34.q_ref.refs_1_, bf16[8,256,256]{2,1,0:T(8,128)(2,1)} %get-tuple-element.46.refs_2_, ...), custom_call_target="tpu_custom_call" | custom-call | flops 8053063680 | bytes 18874368 | tf_op jit(solution)/shard_map/attn_bwd/pallas_call | solution.py:226
  472.7 10.2 %all-gather.11.cloned.1.call-done = bf16[1024,3840]{1,0:T(8,128)(2,1)} async-done(((bf16[128,3840]{1,0:T(8,128)(2,1)}), bf16[1024,3840]{1,0:T(8,128)(2,1)}) %all-gather.11.cloned.1.call-update) | async-done | bytes 7864336 | tf_op jit(solution)/shard_map/all_gather | solution.py:295
  492.5 23.4 %attn_bwd.5 = (bf16[8,128,512]{2,1,0:T(8,128)(2,1)}, bf16[8,3,128,256]{3,2,1,0:T(8,128)(2,1)}, bf16[8,3,128,256]{3,2,1,0:T(8,128)(2,1)}) custom-call(s32[8]{0:T(128)} %get-tuple-element.118.lo_ref.refs_0_, bf16[8,3,128,512]{3,2,1,0:T(8,128)(2,1)} %get-tuple-element.34.q_ref.refs_1_, bf16[8,256,256]{2,1,0:T(8,128)(2,1)} %get-tuple-element.52.refs_2_, ...), custom_call_target="tpu_custom_call" | custom-call | flops 8053063680 | bytes 18874368 | tf_op jit(solution)/shard_map/attn_bwd/pallas_call | solution.py:226
  526.5 12.6 %convolution_convert_fusion = bf16[1024,3840]{1,0:T(8,128)(2,1)} fusion(bf16[1024,1024]{1,0:T(8,128)(2,1)S(1)} %bitcast.119, bf16[3840,256]{1,0:T(8,128)(2,1)S(1)} %bitcast.123, bf16[3840,256]{1,0:T(8,128)(2,1)} %bitcast.124, bf16[3840,512]{1,0:T(8,128)(2,1)S(1)} %bitcast.110), kind=kOutput, calls=%fused_computation.3 | convolution fusion | flops 8080588800 | bytes 17825792 | tf_op jit(solution)/shard_map/dot_general | solution.py:244
  539.2 13.9 %convolution_convert_fusion.2 = bf16[1024,3840]{1,0:T(8,128)(2,1)} fusion(bf16[1024,1024]{1,0:T(8,128)(2,1)} %bitcast.118, bf16[3840,256]{1,0:T(8,128)(2,1)} %bitcast.120, bf16[3840,256]{1,0:T(8,128)(2,1)} %bitcast.125, bf16[3840,512]{1,0:T(8,128)(2,1)} %bitcast.108), kind=kOutput, calls=%fused_computation.5 | convolution fusion | flops 8080588800 | bytes 17825792 | tf_op jit(solution)/shard_map/dot_general | solution.py:244
  553.2 13.2 %convolution_convert_fusion.1 = bf16[1024,3840]{1,0:T(8,128)(2,1)} fusion(bf16[1024,1024]{1,0:T(8,128)(2,1)S(1)} %bitcast.117, bf16[3840,256]{1,0:T(8,128)(2,1)} %bitcast.121, bf16[3840,256]{1,0:T(8,128)(2,1)} %bitcast.126, bf16[3840,512]{1,0:T(8,128)(2,1)} %bitcast.109), kind=kOutput, calls=%fused_computation.4 | convolution fusion | flops 8080588800 | bytes 17825792 | tf_op jit(solution)/shard_map/dot_general | solution.py:244
  576.6 31.8 %fusion.39 = f32[3840,1024]{0,1:T(8,128)S(1)} fusion(bf16[3072,3840]{1,0:T(8,128)(2,1)} %all-gather.5.cloned.1.call-done, bf16[3072,1024]{1,0:T(8,128)(2,1)} %bitcast.112), kind=kOutput, calls=%fused_computation.105 | convolution fusion | flops 24159191040 | bytes 45613056 | tf_op jit(solution)/shard_map/dot_general | solution.py:244
  624.8 12.5 %copy.36 = f32[3840,2,256]{2,1,0:T(2,128)} copy(f32[3840,2,256]{0,2,1:T(8,128)} %bitcast.106) | data formatting | bytes 15728640
  660.1 10.5 %add_add_fusion.1 = f32[512,3840]{1,0:T(8,128)} fusion(f32[512,3840]{1,0:T(8,128)S(1)} %fusion.40, f32[512,3840]{1,0:T(8,128)S(1)} %fusion.41, bf16[1024,512]{1,0:T(8,128)(2,1)S(1)} %bitcast.133, bf16[1024,3840]{1,0:T(8,128)(2,1)} %all-gather.11.cloned.1.call-done), kind=kOutput, calls=%fused_computation.2 | convolution fusion | flops 4030464000 | bytes 32505856 | tf_op jit(solution)/shard_map/dot_general | solution.py:244
  670.6 11.8 %reduce-scatter.15.cloned.1.call-done = bf16[128,3840]{1,0:T(8,128)(2,1)} async-done(((bf16[1024,3840]{1,0:T(8,128)(2,1)}), bf16[128,3840]{1,0:T(8,128)(2,1)}) %reduce-scatter.15.cloned.1.call-update) | async-done | bytes 983056 | tf_op jit(solution)/shard_map/reduce_scatter | solution.py:310
  686.0 22.3 %all-reduce = (f32[3840]{0:T(1024)}, f32[3840]{0:T(1024)}) all-reduce(f32[3840]{0:T(1024)S(1)} %get-tuple-element.84, f32[3840]{0:T(1024)S(1)} %add_add_fusion.5), channel_id=1, replica_groups=mesh['dp'=4,'tp'=8] {'tp'}, use_global_device_ids=true, to_apply=%region_16.0 | all-reduce | flops 7680 | bytes 61440 | tf_op jit(solution)/shard_map/psum | solution.py:319
  (127 shorter events, 150.9 us)
Async XLA Ops:
  7.2 121.5 %all-gather.5.cloned.1.call-start = ((), (), s32[]{:S(2)}) async-start(), calls=%async_computation.6 | async-start | bytes 26542080 | tf_op jit(solution)/shard_map/all_gather | solution.py:269
  14.4 228.6 %reduce-scatter.7.cloned.1.call-start = ((), (), s32[]{:S(2)}) async-start(), calls=%async_computation.7 | async-start | bytes 8847360 | tf_op jit(solution)/shard_map/reduce_scatter | solution.py:287
  29.8 12.0 %copy-start.12 = (bf16[3840,1,256]{2,0,1:T(8,128)(2,1)S(1)}, bf16[3840,1,256]{2,0,1:T(8,128)(2,1)}, u32[]{:S(2)}) copy-start(bf16[3840,1,256]{2,0,1:T(8,128)(2,1)} %param.14) | copy-start | bytes 5898244
  29.8 12.0 %copy-start.14 = (bf16[3840,1,256]{2,0,1:T(8,128)(2,1)S(1)}, bf16[3840,1,256]{2,0,1:T(8,128)(2,1)}, u32[]{:S(2)}) copy-start(bf16[3840,1,256]{2,0,1:T(8,128)(2,1)} %param.13) | copy-start | bytes 5898244
  32.7 9.0 %copy-start.4 = (bf16[480,8,2,256]{3,1,2,0:T(8,128)(2,1)}, bf16[480,8,2,256]{3,1,2,0:T(8,128)(2,1)S(1)}, u32[]{:S(2)}) copy-start(bf16[480,8,2,256]{3,1,2,0:T(8,128)(2,1)S(1)} %copy.39) | copy-start | bytes 11796484
  189.7 95.0 %reduce-scatter.9.cloned.1.call-start = ((), (), s32[]{:S(2)}) async-start(), calls=%async_computation.8 | async-start | bytes 8847360 | tf_op jit(solution)/shard_map/reduce_scatter | solution.py:287
  217.4 116.6 %reduce-scatter.11.cloned.1.call-start = ((), (), s32[]{:S(2)}) async-start(), calls=%async_computation.9 | async-start | bytes 8847360 | tf_op jit(solution)/shard_map/reduce_scatter | solution.py:287
  242.3 148.7 %all-gather.7.cloned.1.call-start = ((), (), s32[]{:S(2)}) async-start(), calls=%async_computation.10 | async-start | bytes 8847360 | tf_op jit(solution)/shard_map/all_gather | solution.py:295
  334.1 7.9 %copy-start.3 = (bf16[1,384,3840]{2,1,0:T(8,128)(2,1)S(1)}, bf16[1,384,3840]{2,1,0:T(8,128)(2,1)}, u32[]{:S(2)}) copy-start(bf16[1,384,3840]{2,1,0:T(8,128)(2,1)} %param.11) | copy-start | bytes 8847364
  334.1 7.9 %copy-start.6 = (bf16[128,3840]{1,0:T(8,128)(2,1)S(1)}, bf16[128,3840]{1,0:T(8,128)(2,1)}, u32[]{:S(2)}) copy-start(bf16[128,3840]{1,0:T(8,128)(2,1)} %reduce-scatter.7.cloned.1.call-done) | copy-start | bytes 2949124
  334.1 7.9 %copy-start.7 = (bf16[128,3840]{1,0:T(8,128)(2,1)S(1)}, bf16[128,3840]{1,0:T(8,128)(2,1)}, u32[]{:S(2)}) copy-start(bf16[128,3840]{1,0:T(8,128)(2,1)} %reduce-scatter.9.cloned.1.call-done) | copy-start | bytes 2949124
  334.1 7.9 %copy-start.8 = (bf16[128,3840]{1,0:T(8,128)(2,1)S(1)}, bf16[128,3840]{1,0:T(8,128)(2,1)}, u32[]{:S(2)}) copy-start(bf16[128,3840]{1,0:T(8,128)(2,1)} %reduce-scatter.11.cloned.1.call-done) | copy-start | bytes 2949124
  346.2 90.7 %all-gather.9.cloned.1.call-start = ((), (), s32[]{:S(2)}) async-start(), calls=%async_computation.11 | async-start | bytes 8847360 | tf_op jit(solution)/shard_map/all_gather | solution.py:295
  346.8 136.1 %all-gather.11.cloned.1.call-start = ((), (), s32[]{:S(2)}) async-start(), calls=%async_computation.12 | async-start | bytes 8847360 | tf_op jit(solution)/shard_map/all_gather | solution.py:295
  347.6 322.9 %reduce-scatter.17.cloned.1.call-start = ((), (), s32[]{:S(2)}) async-start(), calls=%async_computation.15 | async-start | bytes 8847360 | tf_op jit(solution)/shard_map/reduce_scatter | solution.py:310
  492.5 23.4 %copy-start.18 = (bf16[8,128,512]{2,1,0:T(8,128)(2,1)S(1)}, bf16[8,128,512]{2,1,0:T(8,128)(2,1)}, u32[]{:S(2)}) copy-start(bf16[8,128,512]{2,1,0:T(8,128)(2,1)} %get-tuple-element.45) | copy-start | bytes 3145732
  492.5 23.4 %copy-start.19 = (bf16[8,128,512]{2,1,0:T(8,128)(2,1)S(1)}, bf16[8,128,512]{2,1,0:T(8,128)(2,1)}, u32[]{:S(2)}) copy-start(bf16[8,128,512]{2,1,0:T(8,128)(2,1)} %get-tuple-element.51) | copy-start | bytes 3145732
  539.2 131.4 %reduce-scatter.13.cloned.1.call-start = ((), (), s32[]{:S(2)}) async-start(), calls=%async_computation.13 | async-start | bytes 8847360 | tf_op jit(solution)/shard_map/reduce_scatter | solution.py:310
  553.2 129.2 %reduce-scatter.15.cloned.1.call-start = ((), (), s32[]{:S(2)}) async-start(), calls=%async_computation.14 | async-start | bytes 8847360 | tf_op jit(solution)/shard_map/reduce_scatter | solution.py:310
  637.3 9.1 %copy-start.15 = (bf16[8,128,512]{2,1,0:T(8,128)(2,1)S(1)}, bf16[8,128,512]{2,1,0:T(8,128)(2,1)}, u32[]{:S(2)}) copy-start(bf16[8,128,512]{2,1,0:T(8,128)(2,1)} %get-tuple-element.37) | copy-start | bytes 3145732
  660.0 22.3 %copy-start.1 = (bf16[1,384,3840]{2,1,0:T(8,128)(2,1)S(1)}, bf16[1,384,3840]{2,1,0:T(8,128)(2,1)}, u32[]{:S(2)}) copy-start(bf16[1,384,3840]{2,1,0:T(8,128)(2,1)} %param.9) | copy-start | bytes 8847364
  660.0 22.3 %copy-start.21 = (f32[3840]{0:T(1024)S(1)}, f32[3840]{0:T(1024)}, u32[]{:S(2)}) copy-start(f32[3840]{0:T(1024)} %copy-done.20) | copy-start | bytes 46084
  660.0 22.3 %copy-start.23 = (f32[384]{0:T(512)S(1)}, f32[384]{0:T(512)}, u32[]{:S(2)}) copy-start(f32[384]{0:T(512)} %copy-done.22) | copy-start | bytes 4612
  670.5 15.4 %copy-start.25 = (f32[384]{0:T(512)S(1)}, f32[384]{0:T(512)}, u32[]{:S(2)}) copy-start(f32[384]{0:T(512)} %copy-done.24) | copy-start | bytes 4612
  (14 other events, 43.0 us)
Sparse Core Ops, SparseCore 0:
  14.5 114.1 all-gather.4
  189.8 45.8 reduce-scatter.6
  238.1 46.5 reduce-scatter.8
  287.4 46.5 reduce-scatter.10
  346.3 44.6 all-gather.6
  392.5 44.3 all-gather.8
  438.5 44.3 all-gather.10
  539.3 45.2 reduce-scatter.16
  586.9 46.5 reduce-scatter.12
  635.7 46.5 reduce-scatter.14

commit v2 on v0

v2 whole, which is shorter than its diff:
```python
import functools

import jax
import jax.numpy as jnp
from jax import lax
from jax.experimental import pallas as pl
from jax.experimental.pallas import tpu as pltpu
from jax.sharding import PartitionSpec as P

WINDOW = 4096
SOFT_CAP = 50.0
NORM_EPS = 1e-6
ROPE_THETA = 10000.0
ROWS = 128
LOG2E = 1.4426950408889634
VMEM_LIMIT = 60 * 1024 * 1024
KEY_BLOCKS = 3


def rms_norm(hidden, scale_w):
    values = hidden.astype(jnp.float32)
    inv_rms = lax.rsqrt(jnp.mean(values * values, axis=-1, keepdims=True) + NORM_EPS)
    return (values * inv_rms * (1.0 + scale_w)).astype(jnp.bfloat16)


def params(n=1):
    return pltpu.CompilerParams(dimension_semantics=("arbitrary",) * n, vmem_limit_bytes=VMEM_LIMIT)


def key_mask(posq_ref, posk_ref, start, limit):
    keys = KEY_BLOCKS * ROWS
    gap = posq_ref[0, 0] - posk_ref[pl.ds(start, KEY_BLOCKS)].reshape(keys, ROWS)
    row = lax.broadcasted_iota(jnp.int32, (keys, ROWS), 0)
    return (gap >= 0) & (gap < WINDOW) & (row < limit)


def key_range(lo_ref, own, cur, n_chunks):
    end = own * n_chunks + cur + 1
    steps = (end - lo_ref[end - 1] + KEY_BLOCKS - 1) // KEY_BLOCKS

    def at(i):
        stop = end - KEY_BLOCKS * i
        start = jnp.maximum(stop - KEY_BLOCKS, 0)
        return start, (stop - start) * ROWS

    return steps, at


def side_by_side(ref, start):
    return jnp.concatenate([ref[start + c] for c in range(KEY_BLOCKS)], axis=1)


def masked_exp(t, mask, n_heads):
    e = jnp.exp2(t * (SOFT_CAP * LOG2E))
    return jnp.concatenate([jnp.where(mask, e[:, h * ROWS:(h + 1) * ROWS], 0.0) for h in range(n_heads)], axis=1)


def fwd_kernel(n_heads, lo_ref, q_ref, k_ref, vt_ref, posq_ref, posk_ref, o_ref, ot_ref, qt_ref, li_ref, acc_ref):
    own, cur = pl.program_id(0), pl.program_id(1)
    n_chunks, hd = pl.num_programs(1), k_ref.shape[2]
    keys = KEY_BLOCKS * ROWS
    q = q_ref[0, 0]
    qt = jnp.concatenate([q[:, h * hd:(h + 1) * hd].T for h in range(n_heads)], axis=1)
    qt_ref[0, 0] = qt
    acc_ref[...] = jnp.zeros_like(acc_ref)

    steps, at = key_range(lo_ref, own, cur, n_chunks)

    def body(i, l_sum):
        start, limit = at(i)
        k_b = k_ref[pl.ds(start, KEY_BLOCKS)].reshape(keys, hd)
        s = jnp.dot(k_b, qt_ref[0, 0], preferred_element_type=jnp.float32)
        t = jnp.tanh(s * (1.0 / SOFT_CAP))
        e = masked_exp(t, key_mask(posq_ref, posk_ref, start, limit), n_heads)
        acc_ref[...] += jnp.dot(side_by_side(vt_ref, start), e.astype(jnp.bfloat16), preferred_element_type=jnp.float32)
        return l_sum + jnp.sum(e, axis=0, keepdims=True)

    l_sum = lax.fori_loop(0, steps, body, jnp.zeros((1, n_heads * ROWS), jnp.float32))
    inv = 1.0 / l_sum
    li_ref[0, 0] = inv
    ot = (acc_ref[...] * inv).astype(jnp.bfloat16)
    ot_ref[0, 0] = ot
    for h in range(n_heads):
        o_ref[0, 0, :, h * hd:(h + 1) * hd] = ot[:, h * ROWS:(h + 1) * ROWS].T


def attn_fwd(n_heads, lo, q, k, vt, posq, posk):
    n_own, n_chunks, rows = q.shape[:3]
    hd = k.shape[-1]
    lanes = n_heads * rows
    full = lambda x: pl.BlockSpec(x.shape, lambda i, c, lo: (0,) * x.ndim)
    per = lambda s: pl.BlockSpec((1, 1) + s, lambda i, c, lo: (i, c, 0, 0))
    out = lambda s, t: jax.ShapeDtypeStruct((n_own, n_chunks) + s, t)
    return pl.pallas_call(
        functools.partial(fwd_kernel, n_heads),
        grid_spec=pltpu.PrefetchScalarGridSpec(
            num_scalar_prefetch=1, grid=(n_own, n_chunks),
            in_specs=[per((rows, n_heads * hd)), full(k), full(vt), per((1, rows)), full(posk)],
            out_specs=[per((rows, n_heads * hd)), per((hd, lanes)), per((hd, lanes)), per((1, lanes))],
            scratch_shapes=[pltpu.VMEM((hd, lanes), jnp.float32)]),
        out_shape=[out((rows, n_heads * hd), jnp.bfloat16), out((hd, lanes), jnp.bfloat16),
                   out((hd, lanes), jnp.bfloat16), out((1, lanes), jnp.float32)],
        compiler_params=params(2),
        cost_estimate=pl.CostEstimate(flops=2 * q.size * n_own * n_chunks * rows, transcendentals=0, bytes_accessed=12 * k.size),
        name="attn_fwd",
    )(lo, q, k, vt, posq, posk)


def bwd_kernel(n_heads, scale, lo_ref, q_ref, qt_ref, ot_ref, li_ref, do_ref, k_ref, kt_ref, v_ref, posq_ref, posk_ref,
               cos_ref, sin_ref, out_ref, dk_ref, dv_ref, dqt_ref, dot_ref, dos_ref, qs_ref):
    own, cur = pl.program_id(0), pl.program_id(1)
    n_own, n_chunks, hd = pl.num_programs(0), pl.num_programs(1), k_ref.shape[2]
    keys = KEY_BLOCKS * ROWS
    half = hd // 2
    qw = n_heads * hd

    @pl.when((own == 0) & (cur == 0))
    def _():
        dk_ref[...] = jnp.zeros_like(dk_ref)
        dv_ref[...] = jnp.zeros_like(dv_ref)

    do = do_ref[0, 0]
    q = q_ref[0, 0]
    for h in range(n_heads):
        dos_ref[h * ROWS:(h + 1) * ROWS] = do[:, h * hd:(h + 1) * hd]
        qs_ref[h * ROWS:(h + 1) * ROWS] = q[:, h * hd:(h + 1) * hd]
        dot_ref[:, h * ROWS:(h + 1) * ROWS] = do[:, h * hd:(h + 1) * hd].T
    delta = jnp.sum(dot_ref[...].astype(jnp.float32) * ot_ref[0, 0].astype(jnp.float32), axis=0, keepdims=True)
    inv = li_ref[0, 0]
    dqt_ref[...] = jnp.zeros_like(dqt_ref)

    steps, at = key_range(lo_ref, own, cur, n_chunks)

    def body(i, carry):
        start, limit = at(i)
        here = pl.ds(start, KEY_BLOCKS)
        k_b = k_ref[here].reshape(keys, hd)
        v_b = v_ref[here].reshape(keys, hd)
        s = jnp.dot(k_b, qt_ref[0, 0], preferred_element_type=jnp.float32)
        dp = jnp.dot(v_b, dot_ref[...], preferred_element_type=jnp.float32)
        t = jnp.tanh(s * (1.0 / SOFT_CAP))
        p = masked_exp(t, key_mask(posq_ref, posk_ref, start, limit), n_heads) * inv
        ds = (p * (dp - delta) * (1.0 - t * t)).astype(jnp.bfloat16)
        dv_ref[here] += jnp.dot(p.astype(jnp.bfloat16), dos_ref[...], preferred_element_type=jnp.float32).reshape(KEY_BLOCKS, ROWS, hd)
        dk_ref[here] += jnp.dot(ds, qs_ref[...], preferred_element_type=jnp.float32).reshape(KEY_BLOCKS, ROWS, hd)
        dqt_ref[...] += jnp.dot(side_by_side(kt_ref, start), ds, preferred_element_type=jnp.float32)
        return carry

    lax.fori_loop(0, steps, body, 0)

    def unrope(grad, cos, sin):
        lo, hi = grad[:, :half], grad[:, half:]
        return lo * cos + hi * sin, hi * cos - lo * sin

    cos, sin = cos_ref[own, cur], sin_ref[own, cur]
    for h in range(n_heads):
        lo, hi = unrope(dqt_ref[:, h * ROWS:(h + 1) * ROWS].T, cos, sin)
        out_ref[own, cur, :, h * hd:h * hd + half] = (lo * scale).astype(jnp.bfloat16)
        out_ref[own, cur, :, h * hd + half:(h + 1) * hd] = (hi * scale).astype(jnp.bfloat16)

    @pl.when((own == n_own - 1) & (cur == n_chunks - 1))
    def _():
        def fin(i, carry):
            for c in range(out_ref.shape[1]):
                b = i * out_ref.shape[1] + c
                lo, hi = unrope(dk_ref[b], cos_ref[i, c], sin_ref[i, c])
                out_ref[i, c, :, qw:qw + half] = lo.astype(jnp.bfloat16)
                out_ref[i, c, :, qw + half:qw + hd] = hi.astype(jnp.bfloat16)
                out_ref[i, c, :, qw + hd:] = dv_ref[b].astype(jnp.bfloat16)
            return carry
        lax.fori_loop(0, n_own, fin, 0)


def attn_bwd(n_heads, scale, lo, q, qt, ot, li, do, k, kt, v, posq, posk, cos_t, sin_t):
    n_own, n_chunks, rows = q.shape[:3]
    hd = k.shape[-1]
    lanes = n_heads * rows
    once = dict(pipeline_mode=pl.Buffered(1))
    full = lambda x: pl.BlockSpec(x.shape, lambda i, c, lo: (0,) * x.ndim, **once)
    per = lambda s: pl.BlockSpec((1, 1) + s, lambda i, c, lo: (i, c, 0, 0))
    out = jax.ShapeDtypeStruct((n_own, n_chunks, rows, (n_heads + 2) * hd), jnp.bfloat16)
    acc = pltpu.VMEM(k.shape, jnp.float32)
    return pl.pallas_call(
        functools.partial(bwd_kernel, n_heads, scale),
        grid_spec=pltpu.PrefetchScalarGridSpec(
            num_scalar_prefetch=1, grid=(n_own, n_chunks),
            in_specs=[per((rows, n_heads * hd)), per((hd, lanes)), per((hd, lanes)), per((1, lanes)),
                      per((rows, n_heads * hd)), full(k), full(kt), full(v), per((1, rows)), full(posk),
                      full(cos_t), full(sin_t)],
            out_specs=pl.BlockSpec(out.shape, lambda i, c, lo: (0, 0, 0, 0)),
            scratch_shapes=[acc, acc, pltpu.VMEM((hd, lanes), jnp.float32), pltpu.VMEM((hd, lanes), jnp.bfloat16),
                            pltpu.VMEM((lanes, hd), jnp.bfloat16), pltpu.VMEM((lanes, hd), jnp.bfloat16)]),
        out_shape=out,
        compiler_params=params(2),
        cost_estimate=pl.CostEstimate(flops=5 * q.size * n_own * n_chunks * rows, transcendentals=0, bytes_accessed=24 * k.size),
        name="attn_bwd",
    )(lo, q, qt, ot, li, do, k, kt, v, posq, posk, cos_t, sin_t)


MESH = pl.DeviceIdType.MESH


def ring_ids(n):
    me = lax.axis_index('tp')
    return me, me + 1 - 2 * (me % 2), (me + 2) % n, (me + n - 2) % n


def greet(peers):
    barrier = pltpu.get_barrier_semaphore()
    for peer in peers:
        pl.semaphore_signal(barrier, inc=1, device_id={'tp': peer}, device_id_type=MESH)
    pl.semaphore_wait(barrier, len(peers))


def comm_params(cid):
    return pltpu.CompilerParams(collective_id=cid, has_side_effects=True, vmem_limit_bytes=63 * 1024 * 1024)


def gather_ring(n, src_ref, all_ref, send, recv, compute):
    me, partner, right, left = ring_ids(n)
    opp = (me + n // 2) % n
    half = src_ref.shape[0] // 2

    def part(owner, h):
        return all_ref.at[owner, pl.ds(h * half, half)]

    def copy(idx, src, owner, h, target):
        return pltpu.make_async_remote_copy(src_ref=src, dst_ref=part(owner, h), send_sem=send.at[idx], recv_sem=recv.at[idx],
                                            device_id={'tp': target}, device_id_type=MESH)

    def own(idx, h, target):
        return copy(idx, src_ref.at[pl.ds(h * half, half)], me, h, target)

    def fwd(idx, owner, h, target):
        return copy(idx, part(owner, h), owner, h, target)

    def arrived(idx, owner, h):
        fwd(idx, owner, h, partner).wait_recv()

    firsts = [own(0, 0, right), own(2, 1, left), own(1, 1, right), own(3, 0, left), own(4, 0, partner), own(5, 1, partner)]
    for c in firsts:
        c.start()
    all_ref[me] = src_ref[...]
    relays = [fwd(6, left, 0, right), fwd(7, right, 1, left), fwd(8, left, 0, partner), fwd(9, left, 1, partner),
              fwd(10, right, 1, partner), fwd(11, right, 0, partner), fwd(12, opp, 0, partner), fwd(13, opp, 1, partner)]
    l_par, r_par, o_par = (partner + n - 2) % n, (partner + 2) % n, (partner + n // 2) % n
    order = (me, partner, left, right, l_par, r_par, opp, o_par)

    def step(i, carry):
        @pl.when(i == 1)
        def _():
            arrived(4, partner, 0)
            arrived(5, partner, 1)

        @pl.when(i == 2)
        def _():
            arrived(0, left, 0)
            relays[0].start()
            relays[2].start()
            arrived(2, right, 1)
            relays[1].start()
            relays[4].start()
            arrived(1, left, 1)
            relays[3].start()

        @pl.when(i == 3)
        def _():
            arrived(3, right, 0)
            relays[5].start()

        @pl.when(i == 4)
        def _():
            arrived(8, l_par, 0)
            arrived(9, l_par, 1)

        @pl.when(i == 5)
        def _():
            arrived(10, r_par, 1)
            arrived(11, r_par, 0)

        @pl.when(i == 6)
        def _():
            arrived(6, opp, 0)
            relays[6].start()
            arrived(7, opp, 1)
            relays[7].start()

        @pl.when(i == 7)
        def _():
            arrived(12, o_par, 0)
            arrived(13, o_par, 1)

        owner = order[0]
        for j in range(1, len(order)):
            owner = jnp.where(i == j, order[j], owner)
        compute(owner)
        return carry

    lax.fori_loop(0, n, step, 0)
    for c in firsts + relays:
        c.wait_send()


def gather_scratch(n, rows, d_model):
    return [pltpu.VMEM((n, rows, d_model), jnp.bfloat16), pltpu.SemaphoreType.DMA((14,)), pltpu.SemaphoreType.DMA((14,))]


def qkv_kernel(n, n_heads, scale, x_ref, gain_ref, w_ref, cos_ref, sin_ref, a_ref, q_ref, k_ref, kt_ref, v_ref, vt_ref,
               own_ref, all_ref, send, recv, out_sem):
    rows = x_ref.shape[0]
    n_chunks, half = cos_ref.shape[1], cos_ref.shape[3]
    hd = 2 * half
    own_ref[...] = rms_norm(x_ref[...], gain_ref[...])
    _, partner, right, left = ring_ids(n)
    greet((partner, right, left))

    def to_hbm(owner):
        return pltpu.make_async_copy(all_ref.at[owner], a_ref.at[owner], out_sem.at[owner])

    def compute(owner):
        to_hbm(owner).start()
        lin = jnp.dot(all_ref[owner], w_ref[...], preferred_element_type=jnp.float32)
        cos = cos_ref[owner].reshape(rows, half)
        sin = sin_ref[owner].reshape(rows, half)

        def rope(col):
            lo = lin[:, col:col + half]
            hi = lin[:, col + half:col + hd]
            return lo * cos - hi * sin, hi * cos + lo * sin

        for h in range(n_heads):
            lo, hi = rope(h * hd)
            q_ref[owner, :, :, h * hd:h * hd + half] = (lo * scale).astype(jnp.bfloat16).reshape(n_chunks, ROWS, half)
            q_ref[owner, :, :, h * hd + half:(h + 1) * hd] = (hi * scale).astype(jnp.bfloat16).reshape(n_chunks, ROWS, half)
        lo, hi = rope(n_heads * hd)
        k = jnp.concatenate([lo.astype(jnp.bfloat16), hi.astype(jnp.bfloat16)], axis=1)
        v = lin[:, (n_heads + 1) * hd:].astype(jnp.bfloat16)
        for c in range(n_chunks):
            b = owner * n_chunks + c
            k_c = k[c * ROWS:(c + 1) * ROWS]
            v_c = v[c * ROWS:(c + 1) * ROWS]
            k_ref[b] = k_c
            kt_ref[b] = k_c.T
            v_ref[b] = v_c
            vt_ref[b] = v_c.T

    gather_ring(n, own_ref, all_ref, send, recv, compute)

    def drain(i, carry):
        to_hbm(i).wait()
        return carry

    lax.fori_loop(0, n, drain, 0)


def gather_qkv(n, n_heads, scale, x, gain, w, cos_t, sin_t):
    rows, d_model = x.shape
    n_chunks, hd = cos_t.shape[1], 2 * cos_t.shape[3]
    blocks = n * n_chunks
    bf = lambda s: jax.ShapeDtypeStruct(s, jnp.bfloat16)
    vmem = pl.BlockSpec(memory_space=pltpu.VMEM)
    return pl.pallas_call(
        functools.partial(qkv_kernel, n, n_heads, scale),
        in_specs=[vmem] * 5, out_specs=[pl.BlockSpec(memory_space=pl.ANY)] + [vmem] * 5,
        out_shape=[bf((n, rows, d_model)), bf((n, n_chunks, ROWS, n_heads * hd)),
                   bf((blocks, ROWS, hd)), bf((blocks, hd, ROWS)), bf((blocks, ROWS, hd)), bf((blocks, hd, ROWS))],
        scratch_shapes=[pltpu.VMEM((rows, d_model), jnp.bfloat16)] + gather_scratch(n, rows, d_model) + [pltpu.SemaphoreType.DMA((n,))],
        compiler_params=comm_params(0),
        cost_estimate=pl.CostEstimate(flops=2 * n * x.size * w.shape[1], transcendentals=0, bytes_accessed=4 * n * x.size),
        name="gather_qkv",
    )(x, gain, w, cos_t, sin_t)


def dproj_kernel(n, n_heads, x_ref, wo_ref, ot_ref, do_ref, gwo_ref, all_ref, send, recv):
    n_chunks, hd = ot_ref.shape[1], ot_ref.shape[2]
    _, partner, right, left = ring_ids(n)
    greet((partner, right, left))
    gwo_ref[...] = jnp.zeros_like(gwo_ref)

    def compute(owner):
        dp = all_ref[owner]
        do = lax.dot_general(dp, wo_ref[...], (((1,), (1,)), ((), ())), preferred_element_type=jnp.float32)
        do_ref[owner] = do.astype(jnp.bfloat16).reshape(n_chunks, ROWS, n_heads * hd)
        for h in range(n_heads):
            ot = jnp.concatenate([ot_ref[owner, c, :, h * ROWS:(h + 1) * ROWS] for c in range(n_chunks)], axis=1)
            gwo_ref[h * hd:(h + 1) * hd] += jnp.dot(ot, dp, preferred_element_type=jnp.float32)

    gather_ring(n, x_ref, all_ref, send, recv, compute)


def gather_dproj(n, n_heads, d_proj, wo, ot):
    rows, d_model = d_proj.shape
    n_chunks, hd = ot.shape[1], ot.shape[2]
    vmem = pl.BlockSpec(memory_space=pltpu.VMEM)
    return pl.pallas_call(
        functools.partial(dproj_kernel, n, n_heads),
        in_specs=[vmem] * 3, out_specs=[vmem] * 2,
        out_shape=[jax.ShapeDtypeStruct((n, n_chunks, ROWS, n_heads * hd), jnp.bfloat16),
                   jax.ShapeDtypeStruct((n_heads * hd, d_model), jnp.float32)],
        scratch_shapes=gather_scratch(n, rows, d_model),
        compiler_params=comm_params(1),
        cost_estimate=pl.CostEstimate(flops=4 * n * rows * d_model * n_heads * hd, transcendentals=0, bytes_accessed=2 * n * d_proj.size),
        name="gather_dproj",
    )(d_proj, wo, ot)


def scatter_kernel(n, trans, pieces, n_heads, *refs):
    if n_heads:
        lhs_ref, rhs_ref, a_ref, out_ref, gq_ref, gk_ref, gv_ref = refs[:7]
        a_buf, g_bufs, a_sem, g_sem = refs[-6], refs[-5:-2], refs[-2], refs[-1]
        acc, pst, pin, rcv, p_send, p_recv, r_send, r_recv = refs[7:-6]
    else:
        lhs_ref, rhs_ref, out_ref, acc, pst, pin, rcv, p_send, p_recv, r_send, r_recv = refs
    me, partner, right, left = ring_ids(n)
    core = me % 2
    chips = n // 2
    chip = me // 2
    width = acc.shape[2]
    rows = acc.shape[1]
    prow = rows // pieces
    hop = (right, left)
    greet((partner, right, left))

    if n_heads:
        tile = a_buf.shape[2]
        hd = gk_ref.shape[2]
        tiles = a_ref.shape[1] // tile
        per_stage = tiles // (chips - 1)
        depth = lhs_ref.shape[2]

        def a_in(t):
            return pltpu.make_async_copy(a_ref.at[:, pl.ds(pl.multiple_of(t * tile, tile), tile)], a_buf.at[t % 2], a_sem.at[t % 2])

        def g_out(t):
            at = pl.ds(pl.multiple_of(t * tile, tile), tile)
            return [pltpu.make_async_copy(b.at[t % 2], g.at[at], g_sem.at[t % 2, i])
                    for i, (b, g) in enumerate(zip(g_bufs, (gq_ref, gk_ref, gv_ref)))]

        def wgrad(t, carry):
            a_in(t).wait()

            @pl.when(t + 1 < tiles)
            def _():
                a_in(t + 1).start()

            @pl.when(t >= 2)
            def _():
                for c in g_out(t - 2):
                    c.wait()

            g = lax.dot_general(a_buf[t % 2], lhs_ref[...].reshape(n * rows, depth), (((0,), (0,)), ((), ())),
                                preferred_element_type=jnp.float32)
            for h in range(n_heads):
                g_bufs[0][t % 2, :, h, :] = g[:, h * hd:(h + 1) * hd]
            g_bufs[1][t % 2, :, 0, :] = g[:, n_heads * hd:(n_heads + 1) * hd]
            g_bufs[2][t % 2, :, 0, :] = g[:, (n_heads + 1) * hd:]
            for c in g_out(t):
                c.start()
            return carry

        a_in(0).start()

    def partial_sum(owner, d):
        if trans:
            return lax.dot_general(lhs_ref[owner], rhs_ref[d * width:(d + 1) * width], (((1,), (1,)), ((), ())),
                                   preferred_element_type=jnp.float32)
        return jnp.dot(lhs_ref[owner], rhs_ref[:, d * width:(d + 1) * width], preferred_element_type=jnp.float32)

    def to_partner(j, d):
        return pltpu.make_async_remote_copy(src_ref=pst.at[j % 2, d], dst_ref=pin.at[j, d], send_sem=p_send.at[j, d],
                                            recv_sem=p_recv.at[j, d], device_id={'tp': partner}, device_id_type=MESH)

    def to_next(j, d, p):
        at = pl.ds(p * prow, prow)
        return pltpu.make_async_remote_copy(src_ref=pin.at[j, d, at], dst_ref=rcv.at[j, d, at], send_sem=r_send.at[j, d, p],
                                            recv_sem=r_recv.at[j, d, p], device_id={'tp': hop[d]}, device_id_type=MESH)

    def stage(j, carry):
        dest = ((chip + 2 * chips - 1 - j) % chips, (chip + 1 + j) % chips)

        @pl.when(j >= 2)
        def _():
            for d in range(2):
                to_partner(j - 2, d).wait_send()

        for d in range(2):
            pst[j % 2, d] = partial_sum(dest[d] * 2 + 1 - core, d).astype(jnp.bfloat16)
            to_partner(j, d).start()
        for d in range(2):
            acc[d] = partial_sum(dest[d] * 2 + core, d)
        for d in range(2):
            to_partner(j, d).wait_recv()
        for p in range(pieces):
            at = slice(p * prow, (p + 1) * prow)
            for d in range(2):
                @pl.when(j == 0)
                def _():
                    pin[0, d, at] = (acc[d, at] + pin[0, d, at].astype(jnp.float32)).astype(jnp.bfloat16)
                    to_next(0, d, p).start()

                @pl.when((j > 0) & (j < chips - 1))
                def _():
                    to_next(j - 1, d, p).wait_recv()
                    pin[j, d, at] = (acc[d, at] + pin[j, d, at].astype(jnp.float32)
                                     + rcv[j - 1, d, at].astype(jnp.float32)).astype(jnp.bfloat16)
                    to_next(j, d, p).start()

                @pl.when(j == chips - 1)
                def _():
                    to_next(chips - 2, d, p).wait_recv()
                    out_ref[at, d * width:(d + 1) * width] = (
                        acc[d, at] + pin[chips - 1, d, at].astype(jnp.float32)
                        + rcv[chips - 2, d, at].astype(jnp.float32)).astype(jnp.bfloat16)
        if n_heads:
            first = jnp.minimum(j * per_stage, tiles)
            lax.fori_loop(first, jnp.minimum(first + per_stage, tiles), wgrad, 0)
        return carry

    lax.fori_loop(0, chips, stage, 0)
    if n_heads:
        for t in (tiles - 2, tiles - 1):
            for c in g_out(t):
                c.wait()
    for d in range(2):
        for j in (chips - 2, chips - 1):
            to_partner(j, d).wait_send()
        for j in range(chips - 1):
            for p in range(pieces):
                to_next(j, d, p).wait_send()


def matmul_scatter(n, cid, trans, lhs, rhs, a=None, n_heads=0):
    rows, depth = lhs.shape[1:]
    d_model = rhs.shape[0] if trans else rhs.shape[1]
    chips, width, pieces = n // 2, d_model // 2, 3
    vmem = pl.BlockSpec(memory_space=pltpu.VMEM)
    hbm = pl.BlockSpec(memory_space=pl.ANY)
    bf = lambda k: pltpu.VMEM((k, 2, rows, width), jnp.bfloat16)
    dma = pltpu.SemaphoreType.DMA
    out_shape = [jax.ShapeDtypeStruct((rows, d_model), jnp.bfloat16)]
    scratch = [pltpu.VMEM((2, rows, width), jnp.float32), bf(2), bf(chips), bf(chips - 1),
               dma((chips, 2)), dma((chips, 2)), dma((chips - 1, 2, pieces)), dma((chips - 1, 2, pieces))]
    args = [lhs, rhs]
    flops = 2 * n * rows * depth * d_model
    if n_heads:
        hd, tile = depth // (n_heads + 2), 256
        args.append(a)
        out_shape += [jax.ShapeDtypeStruct((d_model, k, hd), jnp.float32) for k in (n_heads, 1, 1)]
        scratch += [pltpu.VMEM((2, n * rows, tile), jnp.bfloat16)]
        scratch += [pltpu.VMEM((2, tile, k, hd), jnp.float32) for k in (n_heads, 1, 1)] + [dma((2,)), dma((2, 3))]
        flops *= 2
    return pl.pallas_call(
        functools.partial(scatter_kernel, n, trans, pieces, n_heads),
        in_specs=[vmem] * 2 + [hbm] * (len(args) - 2), out_specs=[vmem] + [hbm] * (len(out_shape) - 1),
        out_shape=out_shape,
        scratch_shapes=scratch,
        compiler_params=comm_params(cid),
        cost_estimate=pl.CostEstimate(flops=flops, transcendentals=0, bytes_accessed=2 * n * rows * d_model),
        name="matmul_scatter",
    )(*args)


def total_kernel(n, x_ref, out_ref, buf, send, recv):
    me = lax.axis_index('tp')
    peers = [(me + i) % n for i in range(1, n)]
    greet(peers)
    out = [pltpu.make_async_remote_copy(src_ref=x_ref, dst_ref=buf.at[me], send_sem=send.at[i], recv_sem=recv.at[i],
                                        device_id={'tp': peers[i]}, device_id_type=MESH) for i in range(n - 1)]
    for c in out:
        c.start()
    buf[me] = x_ref[...]
    for i in range(n - 1):
        src = (me + n - 1 - i) % n
        pltpu.make_async_remote_copy(src_ref=x_ref, dst_ref=buf.at[src], send_sem=send.at[i], recv_sem=recv.at[i],
                                     device_id={'tp': peers[i]}, device_id_type=MESH).wait_recv()
    total = buf[0]
    for i in range(1, n):
        total = total + buf[i]
    out_ref[...] = total
    for c in out:
        c.wait_send()


def group_total(n, x):
    vmem = pl.BlockSpec(memory_space=pltpu.VMEM)
    return pl.pallas_call(
        functools.partial(total_kernel, n),
        in_specs=[vmem], out_specs=vmem, out_shape=jax.ShapeDtypeStruct(x.shape, x.dtype),
        scratch_shapes=[pltpu.VMEM((n,) + x.shape, x.dtype), pltpu.SemaphoreType.DMA((n - 1,)), pltpu.SemaphoreType.DMA((n - 1,))],
        compiler_params=comm_params(4), name="group_total",
    )(x)


def norm_kernel(post, u_ref, g_ref, x_ref, gain_ref, *outs):
    u = u_ref[...].astype(jnp.float32)
    cot = g_ref[...].astype(jnp.float32)
    gain = 1.0 + gain_ref[...]
    inv = lax.rsqrt(jnp.mean(u * u, axis=-1, keepdims=True) + NORM_EPS)
    xhat = u * inv
    if post:
        y_ref, d_ref, dg_ref = outs
        normed = (xhat * gain).astype(jnp.bfloat16).astype(jnp.float32)
        y_ref[...] = (x_ref[...].astype(jnp.float32) + normed).astype(jnp.bfloat16)
    else:
        d_ref, dg_ref = outs
    scaled = cot * gain
    d_u = (inv * (scaled - xhat * jnp.mean(scaled * xhat, axis=-1, keepdims=True))).astype(jnp.bfloat16)
    if post:
        d_ref[...] = d_u
    else:
        d_ref[...] = (x_ref[...].astype(jnp.float32) + d_u.astype(jnp.float32)).astype(jnp.bfloat16)

    @pl.when(pl.program_id(0) == 0)
    def _():
        dg_ref[...] = jnp.zeros_like(dg_ref)

    dg_ref[...] += jnp.sum(cot * xhat, axis=0, keepdims=True)


def norm_backward(post, u, cot, extra, gain):
    rows, d_model = u.shape
    tile = 64
    spec = pl.BlockSpec((tile, d_model), lambda i: (i, 0))
    one = pl.BlockSpec((1, d_model), lambda i: (0, 0))
    wide = jax.ShapeDtypeStruct(u.shape, jnp.bfloat16)
    return pl.pallas_call(
        functools.partial(norm_kernel, post),
        grid=(rows // tile,),
        in_specs=[spec] * 3 + [one],
        out_specs=[spec] * (2 if post else 1) + [one],
        out_shape=[wide] * (2 if post else 1) + [jax.ShapeDtypeStruct((1, d_model), jnp.float32)],
        compiler_params=params(),
        cost_estimate=pl.CostEstimate(flops=20 * u.size, transcendentals=0, bytes_accessed=10 * u.size),
        name="norm_backward",
    )(u, cot, extra, gain)


def solution(mesh):
    act_spec = P('dp', 'tp', None)
    head_spec = P(None, 'tp', None)
    grad_spec = P('dp', 'tp', None)
    in_specs = (act_spec, P('dp', 'tp'), act_spec, head_spec, head_spec, head_spec, P('tp', None, None), P(None), P(None))
    out_specs = (act_spec, act_spec, grad_spec, grad_spec, grad_spec, P(('dp', 'tp'), None, None), P('dp'), P('dp'))
    n_own = mesh.shape['tp']

    def local_step(x_in, positions, grad_out, w_query, w_key, w_value, w_out, gain_pre, gain_post):
        d_model, n_heads, hd = w_query.shape
        loc = x_in.shape[1]
        n_chunks = loc // ROWS
        scale = hd ** -0.5
        half = hd // 2
        qw = n_heads * hd
        w_cat = jnp.concatenate([w_query.reshape(d_model, qw), w_key.reshape(d_model, hd), w_value.reshape(d_model, hd)], axis=1)
        wo = w_out.reshape(qw, d_model)

        pos = lax.all_gather(positions, 'tp', axis=1, tiled=True).reshape(n_own, n_chunks, ROWS)
        inv_freq = ROPE_THETA ** (-2.0 * jnp.arange(half, dtype=jnp.float32) / hd)
        angles = pos.astype(jnp.float32)[..., None] * inv_freq
        cos_t, sin_t = jnp.cos(angles), jnp.sin(angles)
        pos_k = jnp.broadcast_to(pos.reshape(-1, ROWS, 1), (n_own * n_chunks, ROWS, ROWS))
        k_last = pos[:, :, -1].reshape(-1)
        lo = jnp.sum((pos[:, :, :1] - k_last >= WINDOW).astype(jnp.int32), axis=-1).reshape(-1)
        pos_q = pos[:, :, None]

        a_all, q_all, k_all, kt_all, v_all, vt_all = gather_qkv(n_own, n_heads, scale, x_in[0], gain_pre[None], w_cat, cos_t, sin_t)
        o, ot, qt, li = attn_fwd(n_heads, lo, q_all, k_all, vt_all, pos_q, pos_k)
        r, = matmul_scatter(n_own, 2, False, o.reshape(n_own, loc, qw), wo)
        y_out, d_proj, d_gain_post = norm_backward(True, r, grad_out[0], x_in[0], gain_post[None])
        do, grad_wo = gather_dproj(n_own, n_heads, d_proj, wo, ot)
        dcat = attn_bwd(n_heads, scale, lo, q_all, qt, ot, li, do, k_all, kt_all, v_all, pos_q, pos_k, cos_t, sin_t)
        da, grad_wq, grad_wk, grad_wv = matmul_scatter(n_own, 3, True, dcat.reshape(n_own, loc, qw + 2 * hd), w_cat,
                                                       a_all.reshape(n_own * loc, d_model), n_heads)
        grad_x, d_gain_pre = norm_backward(False, x_in[0], da, grad_out[0], gain_pre[None])
        gains = group_total(n_own, jnp.concatenate([d_gain_pre, d_gain_post], axis=0))
        return (y_out[None], grad_x[None], grad_wq, grad_wk, grad_wv, grad_wo.reshape(n_heads, hd, d_model), gains[0], gains[1])

    return jax.shard_map(local_step, mesh=mesh, in_specs=in_specs, out_specs=out_specs, check_vma=False)
```

time: 1460 us -> 629 us (0.43)
  matrix products: 778 us -> 0 us
  Pallas kernels: 0 us -> 570 us
  waiting for transfers between devices: 325 us -> 0 us
  other arithmetic: 159 us -> 12.9 us
  local copies, waits for them, and re-layouts: 135 us -> 27.9 us
  blocking collectives: 36.2 us -> 13.9 us
    dot_general x180 -> x0, matrix products: 778 us -> none  [the longest x48 126 us: block_probs(): jnp.einsum('bqkgd,bskd->bkgqs', q_blk, k_blk, preferred_element_type=jnp....]
    pallas_call x0 -> x9, Pallas kernels: none -> 570 us  [the longest x2 222 us: matmul_scatter(): pl.pallas_call(functools.partial(scatter_kernel, n, trans, pieces, n_head...]
    all_gather x2 -> x0, waiting for transfers between devices: 204 us -> none  [the longest x1 111 us: local_step(): d_proj_all = lax.all_gather(d_proj, 'tp', axis=1, tiled=True)]
    reduce_scatter x2 -> x0, waiting for transfers between devices: 120 us -> none  [the longest x1 120 us: local_step(): lax.psum_scatter(part_proj.astype(jnp.bfloat16), 'tp', scatter_dimension=...]
    dynamic_update_slice x48 -> x0, local copies, waits for them, and re-layouts: 60.3 us -> none  [block_step(): d_q = lax.dynamic_update_slice_in_dim(d_q, dq_blk, q_start, axis=1)]
    reduce_sum x52 -> x1, other arithmetic: 52.4 us -> 0.22 us  [local_step(): jnp.sum((pos[:, :, :1] - k_last >= WINDOW).astype(jnp.int32), axis=-1)]
    another operation x25 -> x0, other arithmetic: 44.6 us -> none
    unnamed x49 -> x23, local copies, waits for them, and re-layouts: 62.1 us -> 20.7 us
  transfers between devices with their start and end apart: 4 -> 0, of which waited for: 3 -> 0; matrix products, arithmetic and copies ran while one was open for 9% -> 0% of each run, Pallas kernels for 0% -> 0%
where the time goes in v2:
time: 629 us; the launch traced here: 626 us
  Pallas kernels  570 us (91%)
  local copies, waits for them, and re-layouts  27.9 us (4%)
  blocking collectives  13.9 us (2%)
  other arithmetic  12.9 us (2%)
    pallas_call x2, Pallas kernels, matmul_scatter(): pl.pallas_call(functools.partial(scatter_kernel, n, trans, pieces, n_head...  222 us
    pallas_call x1, Pallas kernels, gather_qkv(): pl.pallas_call(functools.partial(qkv_kernel, n, n_heads, scale), in_specs...  118 us
    pallas_call x1, Pallas kernels, gather_dproj(): pl.pallas_call(functools.partial(dproj_kernel, n, n_heads), in_specs=[vme...  117 us
    pallas_call x1, Pallas kernels, attn_bwd(): pl.pallas_call(functools.partial(bwd_kernel, n_heads, scale), grid_spec=p...  49.9 us
    pallas_call x1, Pallas kernels, attn_fwd(): pl.pallas_call(functools.partial(fwd_kernel, n_heads), grid_spec=pltpu.Pr...  36.6 us
    unnamed x23, local copies, waits for them, and re-layouts  20.7 us
    pallas_call x2, Pallas kernels, norm_backward(): pl.pallas_call(functools.partial(norm_kernel, post), grid=(rows // tile,)...  18.3 us
    all_gather x1, blocking collectives, local_step(): lax.all_gather(positions, 'tp', axis=1, tiled=True)  13.9 us

profile of v2, /device:TPU:89, one launch (start us, length us, event | category | flops | bytes accessed | tf_op | source)
XLA Modules:
  0.0 626.0 jit_solution(3698775647911405392)
XLA Ops:
  0.6 13.9 %all_gather.3 = s32[1,3072]{1,0:T(1,128)S(1)} all-gather(s32[1,384]{1,0:T(1,128)} %param.10), channel_id=1, replica_groups=mesh['dp'=4,'tp'=8] {'tp'}, dimensions={1}, use_global_device_ids=true | all-gather | bytes 13824 | tf_op jit(solution)/shard_map/all_gather | solution.py:656
  15.8 1.3 broadcast_in_dim.22.gain_ref
  17.1 1.3 broadcast_in_dim.25.gain_ref
  19.8 1.4 broadcast_in_dim.24.posk_ref
  21.3 6.9 %multiply_sine_fusion = (f32[8,3,128,128]{3,2,1,0:T(8,128)}, f32[8,3,128,128]{3,2,1,0:T(8,128)}) fusion(f32[128]{0:T(128)S(1)} %multiply_power_fusion, f32[8,3,128]{2,1,0:T(4,128)S(1)} %convert_element_type.11), kind=kLoop, calls=%fused_computation.1 | loop fusion | flops 393216 | bytes 3158528 | tf_op jit(solution)/shard_map/sin | solution.py:659
  28.1 0.8 copy.24
  30.3 3.8 pad_maximum_fusion.w_ref.refs_1_
  34.0 117.9 %gather_qkv.1 = (bf16[8,384,3840]{2,1,0:T(8,128)(2,1)}, bf16[8,3,128,512]{3,2,1,0:T(8,128)(2,1)}, bf16[24,128,256]{2,1,0:T(8,128)(2,1)}, bf16[24,256,128]{2,1,0:...) custom-call(bf16[384,3840]{1,0:T(8,128)(2,1)} %bitcast.17, ...), custom_call_target="tpu_custom_call" | custom-call | flops 24159191040 | bytes 47185920 | tf_op jit(solution)/shard_map/gather_qkv/pallas_call | solution.py:362
  152.0 36.6 %attn_fwd.1 = (bf16[8,3,128,512]{3,2,1,0:T(8,128)(2,1)}, bf16[8,3,256,256]{3,2,1,0:T(8,128)(2,1)}, bf16[8,3,256,256]{3,2,1,0:T(8,128)(2,1)}, f32[8,3,1,256]{3,2,1,0:T(1,128)}) custom-call(s32[24]{0:T(128)} %reshape.59.lo_ref, bf16[8,3,128,512]{3,2,1,0:T(8,128)(2,1)} %get-tuple-element.29.q_ref, bf16[24,128,256]{2,1,0:T(8,128)(2,1)} %get-tuple-element.30.k_ref, ...), custom_call_target="tpu_custom_call" | custom-call | flops 9663676416 | bytes 9437184 | tf_op jit(solution)/shard_map/attn_fwd/pallas_call | solution.py:94
  188.6 109.2 %matmul_scatter.2.u_ref = bf16[384,3840]{1,0:T(8,128)(2,1)} custom-call(bf16[8,384,512]{2,1,0:T(8,128)(2,1)} %bitcast.38, bf16[512,3840]{1,0:T(8,128)(2,1)} %bitcast.32), custom_call_target="tpu_custom_call" | custom-call | flops 12079595520 | bytes 23592960 | tf_op jit(solution)/shard_map/matmul_scatter/pallas_call | solution.py:552
  297.9 9.7 %norm_backward.2 = (bf16[384,3840]{1,0:T(8,128)(2,1)}, bf16[384,3840]{1,0:T(8,128)(2,1)}, f32[1,3840]{1,0:T(1,128)}) custom-call(bf16[384,3840]{1,0:T(8,128)(2,1)} %matmul_scatter.2.u_ref, bf16[384,3840]{1,0:T(8,128)(2,1)} %bitcast.20, bf16[384,3840]{1,0:T(8,128)(2,1)} %bitcast.18, f32[1,3840]{1,0:T(1,128)} %broadcast_in_dim.25.gain_ref), custom_call_target="tpu_custom_call" | custom-call | flops 29491200 | bytes 14745600 | tf_op jit(solution)/shard_map/norm_backward/pallas_call | solution.py:626
  307.6 116.6 %gather_dproj.1 = (bf16[8,3,128,512]{3,2,1,0:T(8,128)(2,1)}, f32[512,3840]{1,0:T(8,128)}) custom-call(bf16[384,3840]{1,0:T(8,128)(2,1)} %get-tuple-element.37.x_ref, bf16[512,3840]{1,0:T(8,128)(2,1)} %bitcast.33, bf16[8,3,256,256]{3,2,1,0:T(8,128)(2,1)} %get-tuple-element.35.ot_ref), custom_call_target="tpu_custom_call" | custom-call | flops 24159191040 | bytes 23592960 | tf_op jit(solution)/shard_map/gather_dproj/pallas_call | solution.py:395
  424.2 49.9 %attn_bwd.1 = bf16[8,3,128,1024]{3,2,1,0:T(8,128)(2,1)} custom-call(s32[24]{0:T(128)} %reshape.59.lo_ref, bf16[8,3,128,512]{3,2,1,0:T(8,128)(2,1)} %get-tuple-element.29.q_ref, bf16[8,3,256,256]{3,2,1,0:T(8,128)(2,1)} %get-tuple-element.34.qt_ref, bf16[8,3,256,256]{3,2,1,0:T(8,128)(2,1)} %get-tuple-element.35.ot_ref, ...), custom_call_target="tpu_custom_call" | custom-call | flops 24159191040 | bytes 18874368 | tf_op jit(solution)/shard_map/attn_bwd/pallas_call | solution.py:183
  474.1 113.1 %matmul_scatter.3 = (bf16[384,3840]{1,0:T(8,128)(2,1)}, f32[3840,2,256]{2,1,0:T(2,128)}, f32[3840,1,256]{2,1,0:T(1,128)}, f32[3840,1,256]{2,1,0:T(1,128)}) custom-call(bf16[8,384,1024]{2,1,0:T(8,128)(2,1)} %bitcast.37, bf16[3840,1024]{1,0:T(8,128)(2,1)} %pad_maximum_fusion.w_ref.refs_1_, bf16[3072,3840]{1,0:T(8,128)(2,1)} %bitcast.36), custom_call_target="tpu_custom_call" | custom-call | flops 48318382080 | bytes 23592960 | tf_op jit(solution)/shard_map/matmul_scatter/pallas_call | solution.py:552
  587.3 8.5 %norm_backward.3 = (bf16[384,3840]{1,0:T(8,128)(2,1)}, f32[1,3840]{1,0:T(1,128)}) custom-call(bf16[384,3840]{1,0:T(8,128)(2,1)} %bitcast.19, bf16[384,3840]{1,0:T(8,128)(2,1)} %get-tuple-element.42.g_ref, bf16[384,3840]{1,0:T(8,128)(2,1)} %bitcast.21, f32[1,3840]{1,0:T(1,128)} %broadcast_in_dim.22.gain_ref), custom_call_target="tpu_custom_call" | custom-call | flops 29491200 | bytes 14745600 | tf_op jit(solution)/shard_map/norm_backward/pallas_call | solution.py:626
  595.8 1.4 pad_maximum_fusion.1.x_ref
  597.2 8.7 %group_total.1 = f32[2,3840]{1,0:T(2,128)} custom-call(f32[2,3840]{1,0:T(2,128)} %pad_maximum_fusion.1.x_ref), custom_call_target="tpu_custom_call" | custom-call | tf_op jit(solution)/shard_map/group_total/pallas_call | solution.py:586
  605.9 1.5 slice_reduce_fusion.1
  607.4 9.0 %copy.29 = f32[3840,2,256]{2,1,0:T(2,128)} copy(f32[3840,2,256]{2,1,0:T(2,128)} %get-tuple-element.66) | data formatting | bytes 15728640
  616.5 2.0 copy.30
  618.5 2.0 copy.31
  620.5 1.0 slice-done
  621.5 1.3 slice-done.1
  622.8 3.2 copy.32
  (28 shorter events, 3.9 us)
Async XLA Ops:
  14.6 14.4 %copy-start.5 = (s32[1,3072]{1,0:T(1,128)}, s32[1,3072]{1,0:T(1,128)S(1)}, u32[]{:S(2)}) copy-start(s32[1,3072]{1,0:T(1,128)S(1)} %all_gather.3) | copy-start | bytes 36868
  19.8 8.3 %copy-start = (bf16[3840,2,256]{2,1,0:T(2,128)(2,1)S(1)}, bf16[3840,2,256]{2,1,0:T(2,128)(2,1)}, u32[]{:S(2)}) copy-start(bf16[3840,2,256]{2,1,0:T(2,128)(2,1)} %param.12) | copy-start | bytes 11796484
  28.1 1.5 copy-start.3
  28.1 2.1 copy-start.4
  587.3 8.6 %copy-start.6 = (f32[1,3840]{1,0:T(1,128)S(1)}, f32[1,3840]{1,0:T(1,128)}, u32[]{:S(2)}) copy-start(f32[1,3840]{1,0:T(1,128)} %get-tuple-element.49) | copy-start | bytes 46084
  607.4 9.0 %copy-start.2 = (f32[3840,1,256]{2,1,0:T(1,128)S(1)}, f32[3840,1,256]{2,1,0:T(1,128)}, u32[]{:S(2)}) copy-start(f32[3840,1,256]{2,1,0:T(1,128)} %get-tuple-element.67) | copy-start | bytes 11796484
  607.4 11.0 %copy-start.1 = (f32[3840,1,256]{2,1,0:T(1,128)S(1)}, f32[3840,1,256]{2,1,0:T(1,128)}, u32[]{:S(2)}) copy-start(f32[3840,1,256]{2,1,0:T(1,128)} %get-tuple-element.68) | copy-start | bytes 11796484
  616.5 5.0 slice-start
  618.5 4.3 slice-start.1

commit v3 on v2

--- a/solution.py
+++ b/solution.py
@@ -14,13 +14,17 @@
 ROWS = 128
 LOG2E = 1.4426950408889634
 VMEM_LIMIT = 60 * 1024 * 1024
-KEY_BLOCKS = 3
+KEY_BLOCKS = 4
 
 
 def rms_norm(hidden, scale_w):
     values = hidden.astype(jnp.float32)
     inv_rms = lax.rsqrt(jnp.mean(values * values, axis=-1, keepdims=True) + NORM_EPS)
     return (values * inv_rms * (1.0 + scale_w)).astype(jnp.bfloat16)
+
+
+def as_row(ref):
+    return jnp.concatenate([ref[i:i + 1] for i in range(ref.shape[0])], axis=1)
 
 
 def params(n=1):
@@ -50,8 +54,8 @@
     return jnp.concatenate([ref[start + c] for c in range(KEY_BLOCKS)], axis=1)
 
 
-def masked_exp(t, mask, n_heads):
-    e = jnp.exp2(t * (SOFT_CAP * LOG2E))
+def masked_exp(t, mask, n_heads, shift=0.0):
+    e = jnp.exp2(t * (SOFT_CAP * LOG2E) - shift)
     return jnp.concatenate([jnp.where(mask, e[:, h * ROWS:(h + 1) * ROWS], 0.0) for h in range(n_heads)], axis=1)
 
 
@@ -77,7 +81,7 @@
 
     l_sum = lax.fori_loop(0, steps, body, jnp.zeros((1, n_heads * ROWS), jnp.float32))
     inv = 1.0 / l_sum
-    li_ref[0, 0] = inv
+    li_ref[0, 0] = jnp.log2(l_sum)
     ot = (acc_ref[...] * inv).astype(jnp.bfloat16)
     ot_ref[0, 0] = ot
     for h in range(n_heads):
@@ -126,7 +130,7 @@
         qs_ref[h * ROWS:(h + 1) * ROWS] = q[:, h * hd:(h + 1) * hd]
         dot_ref[:, h * ROWS:(h + 1) * ROWS] = do[:, h * hd:(h + 1) * hd].T
     delta = jnp.sum(dot_ref[...].astype(jnp.float32) * ot_ref[0, 0].astype(jnp.float32), axis=0, keepdims=True)
-    inv = li_ref[0, 0]
+    log_sum = li_ref[0, 0]
     dqt_ref[...] = jnp.zeros_like(dqt_ref)
 
     steps, at = key_range(lo_ref, own, cur, n_chunks)
@@ -139,7 +143,7 @@
         s = jnp.dot(k_b, qt_ref[0, 0], preferred_element_type=jnp.float32)
         dp = jnp.dot(v_b, dot_ref[...], preferred_element_type=jnp.float32)
         t = jnp.tanh(s * (1.0 / SOFT_CAP))
-        p = masked_exp(t, key_mask(posq_ref, posk_ref, start, limit), n_heads) * inv
+        p = masked_exp(t, key_mask(posq_ref, posk_ref, start, limit), n_heads, log_sum)
         ds = (p * (dp - delta) * (1.0 - t * t)).astype(jnp.bfloat16)
         dv_ref[here] += jnp.dot(p.astype(jnp.bfloat16), dos_ref[...], preferred_element_type=jnp.float32).reshape(KEY_BLOCKS, ROWS, hd)
         dk_ref[here] += jnp.dot(ds, qs_ref[...], preferred_element_type=jnp.float32).reshape(KEY_BLOCKS, ROWS, hd)
@@ -305,12 +309,12 @@
     return [pltpu.VMEM((n, rows, d_model), jnp.bfloat16), pltpu.SemaphoreType.DMA((14,)), pltpu.SemaphoreType.DMA((14,))]
 
 
-def qkv_kernel(n, n_heads, scale, x_ref, gain_ref, w_ref, cos_ref, sin_ref, a_ref, q_ref, k_ref, kt_ref, v_ref, vt_ref,
+def qkv_kernel(n, n_heads, scale, x_ref, gain_ref, wq_ref, wk_ref, wv_ref, cos_ref, sin_ref, a_ref, q_ref, k_ref, kt_ref, v_ref, vt_ref,
                own_ref, all_ref, send, recv, out_sem):
     rows = x_ref.shape[0]
     n_chunks, half = cos_ref.shape[1], cos_ref.shape[3]
     hd = 2 * half
-    own_ref[...] = rms_norm(x_ref[...], gain_ref[...])
+    own_ref[...] = rms_norm(x_ref[...], as_row(gain_ref))
     _, partner, right, left = ring_ids(n)
     greet((partner, right, left))
 
@@ -319,22 +323,24 @@
 
     def compute(owner):
         to_hbm(owner).start()
-        lin = jnp.dot(all_ref[owner], w_ref[...], preferred_element_type=jnp.float32)
+        a = all_ref[owner]
+        q_lin = jnp.dot(a, wq_ref[...], preferred_element_type=jnp.float32)
+        k_lin = jnp.dot(a, wk_ref[...], preferred_element_type=jnp.float32)
+        v = jnp.dot(a, wv_ref[...], preferred_element_type=jnp.float32).astype(jnp.bfloat16)
         cos = cos_ref[owner].reshape(rows, half)
         sin = sin_ref[owner].reshape(rows, half)
 
-        def rope(col):
+        def rope(lin, col):
             lo = lin[:, col:col + half]
             hi = lin[:, col + half:col + hd]
             return lo * cos - hi * sin, hi * cos + lo * sin
 
         for h in range(n_heads):
-            lo, hi = rope(h * hd)
+            lo, hi = rope(q_lin, h * hd)
             q_ref[owner, :, :, h * hd:h * hd + half] = (lo * scale).astype(jnp.bfloat16).reshape(n_chunks, ROWS, half)
             q_ref[owner, :, :, h * hd + half:(h + 1) * hd] = (hi * scale).astype(jnp.bfloat16).reshape(n_chunks, ROWS, half)
-        lo, hi = rope(n_heads * hd)
+        lo, hi = rope(k_lin, 0)
         k = jnp.concatenate([lo.astype(jnp.bfloat16), hi.astype(jnp.bfloat16)], axis=1)
-        v = lin[:, (n_heads + 1) * hd:].astype(jnp.bfloat16)
         for c in range(n_chunks):
             b = owner * n_chunks + c
             k_c = k[c * ROWS:(c + 1) * ROWS]
@@ -353,7 +359,7 @@
     lax.fori_loop(0, n, drain, 0)
 
 
-def gather_qkv(n, n_heads, scale, x, gain, w, cos_t, sin_t):
+def gather_qkv(n, n_heads, scale, x, gain, ws, cos_t, sin_t):
     rows, d_model = x.shape
     n_chunks, hd = cos_t.shape[1], 2 * cos_t.shape[3]
     blocks = n * n_chunks
@@ -361,14 +367,14 @@
     vmem = pl.BlockSpec(memory_space=pltpu.VMEM)
     return pl.pallas_call(
         functools.partial(qkv_kernel, n, n_heads, scale),
-        in_specs=[vmem] * 5, out_specs=[pl.BlockSpec(memory_space=pl.ANY)] + [vmem] * 5,
+        in_specs=[vmem] * 7, out_specs=[pl.BlockSpec(memory_space=pl.ANY)] + [vmem] * 5,
         out_shape=[bf((n, rows, d_model)), bf((n, n_chunks, ROWS, n_heads * hd)),
                    bf((blocks, ROWS, hd)), bf((blocks, hd, ROWS)), bf((blocks, ROWS, hd)), bf((blocks, hd, ROWS))],
         scratch_shapes=[pltpu.VMEM((rows, d_model), jnp.bfloat16)] + gather_scratch(n, rows, d_model) + [pltpu.SemaphoreType.DMA((n,))],
         compiler_params=comm_params(0),
-        cost_estimate=pl.CostEstimate(flops=2 * n * x.size * w.shape[1], transcendentals=0, bytes_accessed=4 * n * x.size),
+        cost_estimate=pl.CostEstimate(flops=2 * n * x.size * (n_heads + 2) * hd, transcendentals=0, bytes_accessed=4 * n * x.size),
         name="gather_qkv",
-    )(x, gain, w, cos_t, sin_t)
+    )(x, gain, *ws, cos_t, sin_t)
 
 
 def dproj_kernel(n, n_heads, x_ref, wo_ref, ot_ref, do_ref, gwo_ref, all_ref, send, recv):
@@ -404,11 +410,11 @@
     )(d_proj, wo, ot)
 
 
-def scatter_kernel(n, trans, pieces, n_heads, *refs):
+def scatter_kernel(n, pieces, n_heads, *refs):
     if n_heads:
-        lhs_ref, rhs_ref, a_ref, out_ref, gq_ref, gk_ref, gv_ref = refs[:7]
+        lhs_ref, wq_ref, wk_ref, wv_ref, a_ref, out_ref, gq_ref, gk_ref, gv_ref = refs[:9]
         a_buf, g_bufs, a_sem, g_sem = refs[-6], refs[-5:-2], refs[-2], refs[-1]
-        acc, pst, pin, rcv, p_send, p_recv, r_send, r_recv = refs[7:-6]
+        acc, pst, pin, rcv, p_send, p_recv, r_send, r_recv = refs[9:-6]
     else:
         lhs_ref, rhs_ref, out_ref, acc, pst, pin, rcv, p_send, p_recv, r_send, r_recv = refs
     me, partner, right, left = ring_ids(n)
@@ -461,9 +467,14 @@
         a_in(0).start()
 
     def partial_sum(owner, d):
-        if trans:
-            return lax.dot_general(lhs_ref[owner], rhs_ref[d * width:(d + 1) * width], (((1,), (1,)), ((), ())),
-                                   preferred_element_type=jnp.float32)
+        if n_heads:
+            total, col = None, 0
+            for w_ref in (wq_ref, wk_ref, wv_ref):
+                part = lax.dot_general(lhs_ref[owner, :, col:col + w_ref.shape[1]], w_ref[d * width:(d + 1) * width],
+                                       (((1,), (1,)), ((), ())), preferred_element_type=jnp.float32)
+                total = part if total is None else total + part
+                col += w_ref.shape[1]
+            return total
         return jnp.dot(lhs_ref[owner], rhs_ref[:, d * width:(d + 1) * width], preferred_element_type=jnp.float32)
 
     def to_partner(j, d):
@@ -529,9 +540,8 @@
                 to_next(j, d, p).wait_send()
 
 
-def matmul_scatter(n, cid, trans, lhs, rhs, a=None, n_heads=0):
+def matmul_scatter(n, cid, lhs, weights, d_model, a=None, n_heads=0):
     rows, depth = lhs.shape[1:]
-    d_model = rhs.shape[0] if trans else rhs.shape[1]
     chips, width, pieces = n // 2, d_model // 2, 3
     vmem = pl.BlockSpec(memory_space=pltpu.VMEM)
     hbm = pl.BlockSpec(memory_space=pl.ANY)
@@ -540,7 +550,7 @@
     out_shape = [jax.ShapeDtypeStruct((rows, d_model), jnp.bfloat16)]
     scratch = [pltpu.VMEM((2, rows, width), jnp.float32), bf(2), bf(chips), bf(chips - 1),
                dma((chips, 2)), dma((chips, 2)), dma((chips - 1, 2, pieces)), dma((chips - 1, 2, pieces))]
-    args = [lhs, rhs]
+    args = [lhs, *weights]
     flops = 2 * n * rows * depth * d_model
     if n_heads:
         hd, tile = depth // (n_heads + 2), 256
@@ -550,8 +560,8 @@
         scratch += [pltpu.VMEM((2, tile, k, hd), jnp.float32) for k in (n_heads, 1, 1)] + [dma((2,)), dma((2, 3))]
         flops *= 2
     return pl.pallas_call(
-        functools.partial(scatter_kernel, n, trans, pieces, n_heads),
-        in_specs=[vmem] * 2 + [hbm] * (len(args) - 2), out_specs=[vmem] + [hbm] * (len(out_shape) - 1),
+        functools.partial(scatter_kernel, n, pieces, n_heads),
+        in_specs=[vmem] * (1 + len(weights)) + [hbm] * (len(args) - 1 - len(weights)), out_specs=[vmem] + [hbm] * (len(out_shape) - 1),
         out_shape=out_shape,
         scratch_shapes=scratch,
         compiler_params=comm_params(cid),
@@ -560,41 +570,67 @@
     )(*args)
 
 
-def total_kernel(n, x_ref, out_ref, buf, send, recv):
+def exchange(n, src_ref, buf, send, recv):
     me = lax.axis_index('tp')
     peers = [(me + i) % n for i in range(1, n)]
     greet(peers)
-    out = [pltpu.make_async_remote_copy(src_ref=x_ref, dst_ref=buf.at[me], send_sem=send.at[i], recv_sem=recv.at[i],
-                                        device_id={'tp': peers[i]}, device_id_type=MESH) for i in range(n - 1)]
+
+    def copy(i, slot):
+        return pltpu.make_async_remote_copy(src_ref=src_ref, dst_ref=buf.at[slot], send_sem=send.at[i], recv_sem=recv.at[i],
+                                            device_id={'tp': peers[i]}, device_id_type=MESH)
+
+    out = [copy(i, me) for i in range(n - 1)]
     for c in out:
         c.start()
-    buf[me] = x_ref[...]
+    buf[me] = src_ref[...]
     for i in range(n - 1):
-        src = (me + n - 1 - i) % n
-        pltpu.make_async_remote_copy(src_ref=x_ref, dst_ref=buf.at[src], send_sem=send.at[i], recv_sem=recv.at[i],
-                                     device_id={'tp': peers[i]}, device_id_type=MESH).wait_recv()
+        copy(i, (me + n - 1 - i) % n).wait_recv()
+    for c in out:
+        c.wait_send()
+
+
+def total_kernel(n, a_ref, b_ref, a_out, b_out, src, buf, send, recv):
+    src[0:1] = a_ref[...]
+    src[1:2] = b_ref[...]
+    exchange(n, src, buf, send, recv)
     total = buf[0]
     for i in range(1, n):
         total = total + buf[i]
-    out_ref[...] = total
-    for c in out:
-        c.wait_send()
-
-
-def group_total(n, x):
+    for i in range(a_out.shape[0]):
+        a_out[i:i + 1] = total[0:1, i * 128:(i + 1) * 128]
+        b_out[i:i + 1] = total[1:2, i * 128:(i + 1) * 128]
+
+
+def positions_kernel(n, x_ref, out_ref, buf, send, recv):
+    exchange(n, x_ref, buf, send, recv)
+    out_ref[...] = buf[...]
+
+
+def exchange_call(n, cid, kernel, args, outs, shape, dtype, extra, name):
     vmem = pl.BlockSpec(memory_space=pltpu.VMEM)
+    dma = pltpu.SemaphoreType.DMA((n - 1,))
     return pl.pallas_call(
-        functools.partial(total_kernel, n),
-        in_specs=[vmem], out_specs=vmem, out_shape=jax.ShapeDtypeStruct(x.shape, x.dtype),
-        scratch_shapes=[pltpu.VMEM((n,) + x.shape, x.dtype), pltpu.SemaphoreType.DMA((n - 1,)), pltpu.SemaphoreType.DMA((n - 1,))],
-        compiler_params=comm_params(4), name="group_total",
-    )(x)
+        functools.partial(kernel, n), in_specs=[vmem] * len(args), out_specs=[vmem] * len(outs), out_shape=outs,
+        scratch_shapes=extra + [pltpu.VMEM((n,) + shape, dtype), dma, dma],
+        compiler_params=comm_params(cid), name=name,
+    )(*args)
+
+
+def group_total(n, a, b):
+    shape = (2, a.shape[1])
+    out = jax.ShapeDtypeStruct((a.shape[1] // 128, 128), a.dtype)
+    return exchange_call(n, 4, total_kernel, [a, b], [out] * 2, shape, a.dtype, [pltpu.VMEM(shape, a.dtype)], "group_total")
+
+
+def gather_positions(n, pos):
+    out = jax.ShapeDtypeStruct((n,) + pos.shape, pos.dtype)
+    return exchange_call(n, 5, positions_kernel, [pos], [out], pos.shape, pos.dtype, [], "gather_positions")[0]
 
 
 def norm_kernel(post, u_ref, g_ref, x_ref, gain_ref, *outs):
     u = u_ref[...].astype(jnp.float32)
     cot = g_ref[...].astype(jnp.float32)
-    gain = 1.0 + gain_ref[...]
+    gain = 1.0 + as_row(gain_ref)
     inv = lax.rsqrt(jnp.mean(u * u, axis=-1, keepdims=True) + NORM_EPS)
     xhat = u * inv
     if post:
@@ -626,7 +662,7 @@
     return pl.pallas_call(
         functools.partial(norm_kernel, post),
         grid=(rows // tile,),
-        in_specs=[spec] * 3 + [one],
+        in_specs=[spec] * 3 + [pl.BlockSpec(gain.shape, lambda i: (0, 0))],
         out_specs=[spec] * (2 if post else 1) + [one],
         out_shape=[wide] * (2 if post else 1) + [jax.ShapeDtypeStruct((1, d_model), jnp.float32)],
         compiler_params=params(),
@@ -650,10 +686,10 @@
         scale = hd ** -0.5
         half = hd // 2
         qw = n_heads * hd
-        w_cat = jnp.concatenate([w_query.reshape(d_model, qw), w_key.reshape(d_model, hd), w_value.reshape(d_model, hd)], axis=1)
+        ws = [w_query.reshape(d_model, qw), w_key.reshape(d_model, hd), w_value.reshape(d_model, hd)]
         wo = w_out.reshape(qw, d_model)
 
-        pos = lax.all_gather(positions, 'tp', axis=1, tiled=True).reshape(n_own, n_chunks, ROWS)
+        pos = gather_positions(n_own, positions).reshape(n_own, n_chunks, ROWS)
         inv_freq = ROPE_THETA ** (-2.0 * jnp.arange(half, dtype=jnp.float32) / hd)
         angles = pos.astype(jnp.float32)[..., None] * inv_freq
         cos_t, sin_t = jnp.cos(angles), jnp.sin(angles)
@@ -662,16 +698,16 @@
         lo = jnp.sum((pos[:, :, :1] - k_last >= WINDOW).astype(jnp.int32), axis=-1).reshape(-1)
         pos_q = pos[:, :, None]
 
-        a_all, q_all, k_all, kt_all, v_all, vt_all = gather_qkv(n_own, n_heads, scale, x_in[0], gain_pre[None], w_cat, cos_t, sin_t)
+        a_all, q_all, k_all, kt_all, v_all, vt_all = gather_qkv(n_own, n_heads, scale, x_in[0], gain_pre.reshape(-1, 128), ws, cos_t, sin_t)
         o, ot, qt, li = attn_fwd(n_heads, lo, q_all, k_all, vt_all, pos_q, pos_k)
-        r, = matmul_scatter(n_own, 2, False, o.reshape(n_own, loc, qw), wo)
-        y_out, d_proj, d_gain_post = norm_backward(True, r, grad_out[0], x_in[0], gain_post[None])
+        r, = matmul_scatter(n_own, 2, o.reshape(n_own, loc, qw), [wo], d_model)
+        y_out, d_proj, d_gain_post = norm_backward(True, r, grad_out[0], x_in[0], gain_post.reshape(-1, 128))
         do, grad_wo = gather_dproj(n_own, n_heads, d_proj, wo, ot)
         dcat = attn_bwd(n_heads, scale, lo, q_all, qt, ot, li, do, k_all, kt_all, v_all, pos_q, pos_k, cos_t, sin_t)
-        da, grad_wq, grad_wk, grad_wv = matmul_scatter(n_own, 3, True, dcat.reshape(n_own, loc, qw + 2 * hd), w_cat,
+        da, grad_wq, grad_wk, grad_wv = matmul_scatter(n_own, 3, dcat.reshape(n_own, loc, qw + 2 * hd), ws, d_model,
                                                        a_all.reshape(n_own * loc, d_model), n_heads)
-        grad_x, d_gain_pre = norm_backward(False, x_in[0], da, grad_out[0], gain_pre[None])
-        gains = group_total(n_own, jnp.concatenate([d_gain_pre, d_gain_post], axis=0))
-        return (y_out[None], grad_x[None], grad_wq, grad_wk, grad_wv, grad_wo.reshape(n_heads, hd, d_model), gains[0], gains[1])
+        grad_x, d_gain_pre = norm_backward(False, x_in[0], da, grad_out[0], gain_pre.reshape(-1, 128))
+        sum_pre, sum_post = group_total(n_own, d_gain_pre, d_gain_post)
+        return (y_out[None], grad_x[None], grad_wq, grad_wk, grad_wv, grad_wo.reshape(n_heads, hd, d_model), sum_pre.reshape(-1), sum_post.reshape(-1))
 
     return jax.shard_map(local_step, mesh=mesh, in_specs=in_specs, out_specs=out_specs, check_vma=False)

time: 629 us -> 611 us (0.971); the launches traced: 626 us -> 615 us
  blocking collectives: 13.9 us -> 0 us
  Pallas kernels: 570 us -> 581 us
    all_gather x1 -> x0, blocking collectives: 13.9 us -> none  [local_step(): lax.all_gather(positions, 'tp', axis=1, tiled=True)]
    pallas_call x3 -> x4, Pallas kernels: 231 us -> 239 us  [the longest x2 222 us: matmul_scatter(): pl.pallas_call(functools.partial(scatter_kernel, n, pieces, n_heads), in_...]
    unnamed x23 -> x21, local copies, waits for them, and re-layouts: 20.7 us -> 22.4 us
where the time goes in v3:
time: 611 us; the launch traced here: 615 us
  Pallas kernels  581 us (95%)
  local copies, waits for them, and re-layouts  25.8 us (4%)
  other arithmetic  7.81 us (1%)
    pallas_call x2, Pallas kernels, matmul_scatter(): pl.pallas_call(functools.partial(scatter_kernel, n, pieces, n_heads), in_...  222 us
    pallas_call x1, Pallas kernels, gather_qkv(): pl.pallas_call(functools.partial(qkv_kernel, n, n_heads, scale), in_specs...  118 us
    pallas_call x1, Pallas kernels, gather_dproj(): pl.pallas_call(functools.partial(dproj_kernel, n, n_heads), in_specs=[vme...  117 us
    pallas_call x1, Pallas kernels, attn_bwd(): pl.pallas_call(functools.partial(bwd_kernel, n_heads, scale), grid_spec=p...  53.5 us
    pallas_call x1, Pallas kernels, attn_fwd(): pl.pallas_call(functools.partial(fwd_kernel, n_heads), grid_spec=pltpu.Pr...  36.3 us
    unnamed x21, local copies, waits for them, and re-layouts  22.4 us
    pallas_call x2, Pallas kernels, norm_backward(): pl.pallas_call(functools.partial(norm_kernel, post), grid=(rows // tile,)...  18.1 us
    pallas_call x2, Pallas kernels, exchange_call(): pl.pallas_call(functools.partial(kernel, n), in_specs=[vmem] * len(args),...  16.6 us

profile of v3, /device:TPU:89, one launch (start us, length us, event | category | flops | bytes accessed | tf_op | source)
XLA Modules:
  0.0 615.3 jit_solution(6868354737138621074)
XLA Ops:
  0.6 7.9 %gather_positions.1 = s32[8,1,384]{2,1,0:T(1,128)} custom-call(s32[1,384]{1,0:T(1,128)} %x_ref.1), custom_call_target="tpu_custom_call" | custom-call | tf_op jit(solution)/shard_map/gather_positions/pallas_call | solution.py:612
  8.5 0.7 fusion
  9.6 0.2 convert_reduce_fusion
  9.9 0.6 reshape.72.lo_ref
  10.5 2.3 broadcast_in_dim.16.posk_ref
  12.8 6.9 %multiply_sine_fusion = (f32[8,3,128,128]{3,2,1,0:T(8,128)}, f32[8,3,128,128]{3,2,1,0:T(8,128)}) fusion(f32[128]{0:T(128)S(1)} %multiply_power_fusion, f32[8,3,128]{2,1,0:T(4,128)S(1)} %copy.31), kind=kLoop, calls=%fused_computation | loop fusion | flops 393216 | bytes 3158528 | tf_op jit(solution)/shard_map/sin | solution.py:695
  19.7 2.6 copy.32
  22.3 117.9 %gather_qkv.1 = (bf16[8,384,3840]{2,1,0:T(8,128)(2,1)}, bf16[8,3,128,512]{3,2,1,0:T(8,128)(2,1)}, bf16[24,128,256]{2,1,0:T(8,128)(2,1)}, bf16[24,256,128]{2,1,0:...) custom-call(bf16[384,3840]{1,0:T(8,128)(2,1)} %bitcast.25, f32[30,128]{1,0:T(8,128)} %bitcast.40, ...), custom_call_target="tpu_custom_call" | custom-call | flops 24159191040 | bytes 47185920 | tf_op jit(solution)/shard_map/gather_qkv/pallas_call | solution.py:368
  140.2 36.3 %attn_fwd.1 = (bf16[8,3,128,512]{3,2,1,0:T(8,128)(2,1)}, bf16[8,3,256,256]{3,2,1,0:T(8,128)(2,1)}, bf16[8,3,256,256]{3,2,1,0:T(8,128)(2,1)}, f32[8,3,1,256]{3,2,1,0:T(1,128)}) custom-call(s32[24]{0:T(128)} %reshape.72.lo_ref, bf16[8,3,128,512]{3,2,1,0:T(8,128)(2,1)} %get-tuple-element.31.q_ref, bf16[24,128,256]{2,1,0:T(8,128)(2,1)} %get-tuple-element.32.k_ref, ...), custom_call_target="tpu_custom_call" | custom-call | flops 9663676416 | bytes 9437184 | tf_op jit(solution)/shard_map/attn_fwd/pallas_call | solution.py:98
  176.6 108.8 %matmul_scatter.2.u_ref = bf16[384,3840]{1,0:T(8,128)(2,1)} custom-call(bf16[8,384,512]{2,1,0:T(8,128)(2,1)} %bitcast.54, bf16[512,3840]{1,0:T(8,128)(2,1)} %bitcast.44), custom_call_target="tpu_custom_call" | custom-call | flops 12079595520 | bytes 23592960 | tf_op jit(solution)/shard_map/matmul_scatter/pallas_call | solution.py:562
  285.4 9.6 %norm_backward.2 = (bf16[384,3840]{1,0:T(8,128)(2,1)}, bf16[384,3840]{1,0:T(8,128)(2,1)}, f32[1,3840]{1,0:T(1,128)}) custom-call(bf16[384,3840]{1,0:T(8,128)(2,1)} %matmul_scatter.2.u_ref, bf16[384,3840]{1,0:T(8,128)(2,1)} %bitcast.28, bf16[384,3840]{1,0:T(8,128)(2,1)} %bitcast.26, f32[30,128]{1,0:T(8,128)} %bitcast.39), custom_call_target="tpu_custom_call" | custom-call | flops 29491200 | bytes 14745600 | tf_op jit(solution)/shard_map/norm_backward/pallas_call | solution.py:662
  295.0 116.6 %gather_dproj.1 = (bf16[8,3,128,512]{3,2,1,0:T(8,128)(2,1)}, f32[512,3840]{1,0:T(8,128)}) custom-call(bf16[384,3840]{1,0:T(8,128)(2,1)} %get-tuple-element.39.x_ref, bf16[512,3840]{1,0:T(8,128)(2,1)} %bitcast.45, bf16[8,3,256,256]{3,2,1,0:T(8,128)(2,1)} %get-tuple-element.37.ot_ref), custom_call_target="tpu_custom_call" | custom-call | flops 24159191040 | bytes 23592960 | tf_op jit(solution)/shard_map/gather_dproj/pallas_call | solution.py:401
  411.5 53.5 %attn_bwd.1 = bf16[8,3,128,1024]{3,2,1,0:T(8,128)(2,1)} custom-call(s32[24]{0:T(128)} %reshape.72.lo_ref, bf16[8,3,128,512]{3,2,1,0:T(8,128)(2,1)} %get-tuple-element.31.q_ref, bf16[8,3,256,256]{3,2,1,0:T(8,128)(2,1)} %get-tuple-element.36.qt_ref, bf16[8,3,256,256]{3,2,1,0:T(8,128)(2,1)} %get-tuple-element.37.ot_ref, ...), custom_call_target="tpu_custom_call" | custom-call | flops 24159191040 | bytes 18874368 | tf_op jit(solution)/shard_map/attn_bwd/pallas_call | solution.py:187
  465.1 113.2 %matmul_scatter.3 = (bf16[384,3840]{1,0:T(8,128)(2,1)}, f32[3840,2,256]{2,1,0:T(2,128)}, f32[3840,1,256]{2,1,0:T(1,128)}, f32[3840,1,256]{2,1,0:T(1,128)}) custom-call(bf16[8,384,1024]{2,1,0:T(8,128)(2,1)} %bitcast.53, bf16[3840,512]{1,0:T(8,128)(2,1)} %bitcast.35, bf16[3840,256]{1,0:T(8,128)(2,1)} %bitcast.49, bf16[3840,256]{1,0:T(8,128)(2,1)} %bitcast.51, ...), custom_call_target="tpu_custom_call" | custom-call | flops 48318382080 | bytes 23592960 | tf_op jit(solution)/shard_map/matmul_scatter/pallas_call | solution.py:562
  578.3 8.5 %norm_backward.3 = (bf16[384,3840]{1,0:T(8,128)(2,1)}, f32[1,3840]{1,0:T(1,128)}) custom-call(bf16[384,3840]{1,0:T(8,128)(2,1)} %bitcast.27, bf16[384,3840]{1,0:T(8,128)(2,1)} %get-tuple-element.44.g_ref, bf16[384,3840]{1,0:T(8,128)(2,1)} %bitcast.29, f32[30,128]{1,0:T(8,128)} %bitcast.41), custom_call_target="tpu_custom_call" | custom-call | flops 29491200 | bytes 14745600 | tf_op jit(solution)/shard_map/norm_backward/pallas_call | solution.py:662
  586.8 8.7 %group_total.1 = (f32[30,128]{1,0:T(8,128)}, f32[30,128]{1,0:T(8,128)}) custom-call(f32[1,3840]{1,0:T(1,128)} %get-tuple-element.50.a_ref, f32[1,3840]{1,0:T(1,128)} %get-tuple-element.51.b_ref), custom_call_target="tpu_custom_call" | custom-call | tf_op jit(solution)/shard_map/group_total/pallas_call | solution.py:612
  595.5 9.0 %copy.42 = f32[3840,2,256]{2,1,0:T(2,128)} copy(f32[3840,2,256]{2,1,0:T(2,128)} %get-tuple-element.70) | data formatting | bytes 15728640
  604.6 2.0 copy.43
  606.6 2.0 copy.44
  608.6 1.0 slice-done
  609.6 1.3 slice-done.1
  610.9 3.2 copy.45
  614.1 0.6 copy.46
  614.7 0.6 copy.47
  (19 shorter events, 0.5 us)
Async XLA Ops:
  10.5 9.2 %copy-start = (bf16[3840,2,256]{2,1,0:T(2,128)(2,1)S(1)}, bf16[3840,2,256]{2,1,0:T(2,128)(2,1)}, u32[]{:S(2)}) copy-start(bf16[3840,2,256]{2,1,0:T(2,128)(2,1)} %param.12) | copy-start | bytes 11796484
  595.5 9.0 %copy-start.2 = (f32[3840,1,256]{2,1,0:T(1,128)S(1)}, f32[3840,1,256]{2,1,0:T(1,128)}, u32[]{:S(2)}) copy-start(f32[3840,1,256]{2,1,0:T(1,128)} %get-tuple-element.71) | copy-start | bytes 11796484
  595.5 11.0 %copy-start.1 = (f32[3840,1,256]{2,1,0:T(1,128)S(1)}, f32[3840,1,256]{2,1,0:T(1,128)}, u32[]{:S(2)}) copy-start(f32[3840,1,256]{2,1,0:T(1,128)} %get-tuple-element.72) | copy-start | bytes 11796484
  604.6 5.0 slice-start
  606.6 4.3 slice-start.1
  610.9 3.2 copy-start.4
  610.9 3.8 copy-start.3
